TPU v7x, 256 devices: a whole 4x4x8 slice. The times are simulated.
256 devices in a mesh: lat: 16 (over z, y_lo), lev: 16 (over y_hi, x, core).
Axes of the slice: x: 4, y: 4 (y_hi: 2, y_lo: 2; y = y_hi * 2 + y_lo), z: 8, core: 2. Of those that a mesh axis runs over, the one named last changes fastest.
Arguments:
- tracer: float32 [2, 16, 768, 1152], P(None, 'lev', 'lat'), may hold values from 0.1 to 2
- east_courant: float32 [16, 768, 1152], P('lev', 'lat'), may hold values from -0.8 to 0.8
- north_courant: float32 [16, 768, 1152], P('lev', 'lat'), may hold values from -0.8 to 0.8
- fall_speed: float32 [2, 16, 768, 1152], P(None, 'lev', 'lat'), may hold values from 0.05 to 0.6
Outputs:
- tracer_out: float32 [2, 16, 768, 1152], P(None, 'lev', 'lat')
- deposit: float32 [2, 768, 1152], P(None, 'lat', 'lev')
All inputs are finite; a program needn't handle non-finite values.
Results may differ from a plain program's by a relative error of at most 0.0003.
Values sent between devices are 32-bit elements; how exact they have to be, the bound alone decides.
A program may use at most 64 MiB of HBM per device.

v0:
```python
import jax
import jax.numpy as jnp
from jax import lax
from jax.sharding import PartitionSpec as P

HSUB = 4
SETTLE_SUBSTEPS = 6


def passed_along(block, axis, distance):
    devices = range(lax.axis_size(axis))
    route = [(i - distance, i) for i in devices if i - distance in devices]
    return lax.ppermute(block, axis, route)


def extended_2(block, sides, width):
    for axis, dim in sides:
        count = lax.axis_size(axis)
        forward = [(i, i + 1) for i in range(count - 1)]
        backward = [(target, source) for source, target in forward]
        low = lax.ppermute(
            lax.slice_in_dim(block, block.shape[dim] - width, None, axis=dim), axis, forward
        )
        high = lax.ppermute(lax.slice_in_dim(block, 0, width, axis=dim), axis, backward)
        block = jnp.concatenate([low, block, high], axis=dim)
    return block


def limiter_face_value(outer_west, inner_west, inner_east, outer_east):
    interp = 7.0 / 12.0 * (inner_west + inner_east) - 1.0 / 12.0 * (outer_west + outer_east)
    return jnp.clip(
        interp, jnp.minimum(inner_west, inner_east), jnp.maximum(inner_west, inner_east)
    )


def window_for_cell(source, start, length, axis_dim):
    return lax.slice_in_dim(source, start, start + length, axis=axis_dim)


def sweep(halo_padded_field, courant, axis_dim):
    cells = halo_padded_field.shape[axis_dim] - 6
    faces = limiter_face_value(
        window_for_cell(halo_padded_field, 0, cells + 3, axis_dim),
        window_for_cell(halo_padded_field, 1, cells + 3, axis_dim),
        window_for_cell(halo_padded_field, 2, cells + 3, axis_dim),
        window_for_cell(halo_padded_field, 3, cells + 3, axis_dim),
    )
    middle = window_for_cell(halo_padded_field, 2, cells + 2, axis_dim)
    west_face = window_for_cell(faces, 0, cells + 2, axis_dim)
    east_face = window_for_cell(faces, 1, cells + 2, axis_dim)
    spread = east_face - west_face
    curvature = 6.0 * middle - 3.0 * (west_face + east_face)
    courant_abs = jnp.abs(courant)
    shape_term = 1.0 - 2.0 / 3.0 * courant_abs
    from_west = window_for_cell(east_face, 0, cells + 1, axis_dim) - 0.5 * courant_abs * (
        window_for_cell(spread, 0, cells + 1, axis_dim)
        - shape_term * window_for_cell(curvature, 0, cells + 1, axis_dim)
    )
    from_east = window_for_cell(west_face, 1, cells + 1, axis_dim) + 0.5 * courant_abs * (
        window_for_cell(spread, 1, cells + 1, axis_dim)
        + shape_term * window_for_cell(curvature, 1, cells + 1, axis_dim)
    )
    face_flux_values = courant * jnp.where(courant >= 0, from_west, from_east)
    return window_for_cell(halo_padded_field, 3, cells, axis_dim) - (
        window_for_cell(face_flux_values, 1, cells, axis_dim)
        - window_for_cell(face_flux_values, 0, cells, axis_dim)
    )


def zonal(field, east_courant):
    last_dim = field.ndim - 1
    width = field.shape[last_dim]
    halo_padded_field = jnp.concatenate(
        [
            window_for_cell(field, width - 3, 3, last_dim),
            field,
            window_for_cell(field, 0, 3, last_dim),
        ],
        last_dim,
    )
    cour_dim = east_courant.ndim - 1
    courant = jnp.concatenate(
        [window_for_cell(east_courant, width - 1, 1, cour_dim), east_courant], cour_dim
    )
    return sweep(halo_padded_field, courant, last_dim)


def settle_flat(column_mass, fall_speed):
    deposit = jnp.zeros_like(column_mass[:, 0])
    for settle_substep in range(SETTLE_SUBSTEPS):
        speeds = fall_speed * (1.0 + 0.5 * jnp.tanh(column_mass))
        face_flux_values = speeds * column_mass
        inflow = jnp.concatenate(
            [jnp.zeros_like(face_flux_values[:, :1]), face_flux_values[:, :-1]], 1
        )
        column_mass = column_mass + inflow - face_flux_values
        deposit = deposit + face_flux_values[:, -1]
    return (column_mass, deposit)


def columns_settle(split_portions):
    column_mass, speed_piece = split_portions
    shape_full = column_mass.shape
    flat_shape = (shape_full[0], shape_full[1], shape_full[2] * shape_full[3])
    settled, deposit = settle_flat(column_mass.reshape(flat_shape), speed_piece.reshape(flat_shape))
    returned = lax.all_to_all(
        settled.reshape(shape_full), "lev", split_axis=1, concat_axis=3, tiled=True
    )
    return (returned, deposit.reshape((shape_full[0], shape_full[2], shape_full[3])))


def on_device(tracer, east_courant, north_courant, fall_speed):
    band_rows = tracer.shape[2]
    all_rows = band_rows * lax.axis_size("lat")
    first_row = lax.axis_index("lat") * band_rows
    row_ids = first_row + jnp.arange(band_rows, dtype=jnp.int32)
    north_faces = jnp.where(
        (row_ids == all_rows - 1)[None, :, None], jnp.zeros_like(north_courant), north_courant
    )
    southern_row = passed_along(north_faces[:, band_rows - 1 :, :], "lat", 1)
    face_cour = jnp.concatenate([southern_row, north_faces], 1)
    halo_depth = 3 * HSUB
    bin_count = tracer.shape[0]
    stacked = jnp.concatenate([tracer, east_courant[None], north_faces[None]], 0)
    extended = extended_2(stacked, (("lat", 2),), halo_depth)
    field = extended[:bin_count]
    east_ext = extended[bin_count]
    north_ext = extended[bin_count + 1]
    for settle_substep in range(HSUB):
        height = field.shape[2]
        field = zonal(field, window_for_cell(east_ext, 3 * settle_substep, height, 1))
        cycle_cour = window_for_cell(north_ext, 3 * settle_substep + 2, height - 5, 1)
        field = sweep(field, cycle_cour, 2)
        global_rows = (
            first_row
            - halo_depth
            + 3 * settle_substep
            + 3
            + jnp.arange(height - 6, dtype=jnp.int32)
        )
        inside = (global_rows >= 0) & (global_rows < all_rows)
        field = jnp.where(inside[None, None, :, None], field, jnp.zeros_like(field))
    field, deposit = columns_settle(
        (
            lax.all_to_all(field, "lev", split_axis=3, concat_axis=1, tiled=True),
            lax.all_to_all(fall_speed, "lev", split_axis=3, concat_axis=1, tiled=True),
        )
    )
    field = zonal(field, east_courant)
    halo_padded_field = extended_2(field, (("lat", 2),), 3)
    field = sweep(halo_padded_field, face_cour, 2)
    return (field, deposit)


def solution(mesh):
    in_specs = (
        P(None, "lev", "lat", None),
        P("lev", "lat", None),
        P("lev", "lat", None),
        P(None, "lev", "lat", None),
    )
    out_specs = (P(None, "lev", "lat", None), P(None, "lat", "lev"))
    return jax.shard_map(
        on_device, mesh=mesh, in_specs=in_specs, out_specs=out_specs, check_vma=False
    )
```

profile of v0, /device:TPU:104, one launch (start us, length us, event | category | flops | bytes accessed | tf_op | source)
XLA Modules:
  0.0 143.8 jit_solution(7793444544582302049)
XLA Ops:
  1.2 1.0 fusion.166
  2.2 1.9 %pad_maximum_fusion.7 = (f32[4,1,12,1152]{3,2,1,0:T(8,128)}, f32[4,1,12,1152]{3,2,1,0:T(8,128)}) fusion(f32[1,1,48,1152]{3,2,1,0:T(8,128)S(1)} %fusion.166, f32[1,1,48,1152]{3,2,1,0:T(8,128)} %bitcast.105, f32[2,1,48,1152]{3,2,1,0:T(8,128)} %param.4), kind=kLoop, calls=%fused_computation.238 | loop fusion | flops 221184 | bytes 1327104 | tf_op jit(solution)/shard_map/slice | solution.py:22
  4.2 4.9 %collective-permute-start = (f32[4,1,12,1152]{3,2,1,0:T(8,128)}, f32[4,1,12,1152]{3,2,1,0:T(8,128)S(1)}, u32[]{:S(2)}, u32[]{:S(2)}) collective-permute-start(f32[4,1,12,1152]{3,2,1,0:T(8,128)} %get-tuple-element.18), channel_id=1, source_target_pairs={{0,16},{16,32},{32,48},{48,64},{64,80},{80,96},{96,112},{112,128},... | collective-permute-start | bytes 663560 | tf_op jit(solution)/shard_map/ppermute | solution.py:21
  9.1 1.9 %collective-permute-start.1 = (f32[4,1,12,1152]{3,2,1,0:T(8,128)}, f32[4,1,12,1152]{3,2,1,0:T(8,128)S(1)}, u32[]{:S(2)}, u32[]{:S(2)}) collective-permute-start(f32[4,1,12,1152]{3,2,1,0:T(8,128)} %get-tuple-element.19), channel_id=1, source_target_pairs={{16,0},{32,16},{48,32},{64,48},{80,64},{96,80},{112,96},{128,112},... | collective-permute-start | bytes 663560 | tf_op jit(solution)/shard_map/ppermute | solution.py:24
  11.0 1.1 copy.247
  12.2 2.9 %reshape.763 = f32[16,1,6912]{2,1,0:T(1,128)} reshape(f32[1152,1,2,48]{3,2,1,0:T(2,128)S(1)} %bitcast.112) | data formatting | bytes 884736
  15.0 6.5 %all-to-all-start.1 = ((f32[16,1,6912]{2,1,0:T(1,128)}), f32[16,1,6912]{2,1,0:T(1,128)}, u32[]{:S(2)}, u32[]{:S(2)}) async-start(f32[16,1,6912]{2,1,0:T(1,128)} %reshape.763), calls=%async_computation.1 | async-start | bytes 884736 | tf_op jit(solution)/shard_map/all_to_all | solution.py:146
  22.2 6.8 %collective-permute-start.2 = (f32[1,1,1152]{2,1,0:T(1,128)}, f32[1,1,1152]{2,1,0:T(1,128)}, u32[]{:S(2)}, u32[]{:S(2)}) collective-permute-start(f32[1,1,1152]{2,1,0:T(1,128)} %slice.902), channel_id=1, source_target_pairs={{0,16},{16,32},{32,48},{48,64},{64,80},{80,96},{96,112},{112,128},... | collective-permute-start | bytes 13832 | tf_op jit(solution)/shard_map/ppermute | solution.py:13
  30.8 0.9 abs_multiply_fusion.5
  31.7 0.8 maximum_bitcast_fusion.4
  32.7 0.9 slice.755
  33.7 0.7 fusion.163
  34.4 1.0 abs_multiply_fusion.1
  35.4 0.8 fusion.145
  36.2 1.0 slice_bitcast_fusion.2
  37.3 0.7 compare_bitcast_fusion
  38.0 0.8 fusion.162
  38.7 0.7 fusion.161
  39.4 1.0 abs_multiply_fusion
  40.5 0.8 fusion.144
  41.3 1.0 slice_bitcast_fusion.3
  42.3 0.7 compare_bitcast_fusion.1
  43.0 0.7 fusion.160
  43.7 0.7 fusion.159
  44.4 1.0 abs_multiply_fusion.2
  45.4 0.8 fusion.146
  46.2 1.0 slice_bitcast_fusion.5
  47.2 0.7 compare_bitcast_fusion.3
  47.8 0.7 fusion.158
  48.6 0.9 abs_multiply_fusion.3
  49.6 0.8 fusion.148
  50.3 1.0 slice_bitcast_fusion.4
  51.3 0.7 compare_bitcast_fusion.2
  52.1 1.5 %concatenate.288 = f32[2,1,72,1158]{3,2,1,0:T(8,128)S(1)} concatenate(f32[2,1,72,3]{3,2,1,0:T(8,128)S(1)} %get-tuple-element.15, f32[2,1,72,1152]{3,2,1,0:T(8,128)} %slice.755, f32[2,1,72,3]{3,2,1,0:T(8,128)S(1)} %get-tuple-element.14), dimensions={3} | concatenate | bytes 1334016 | tf_op jit(solution)/shard_map/concatenate | solution.py:73
  53.6 1.9 %fusion.21 = f32[2,1,72,1155]{3,2,1,0:T(8,128)S(1)} fusion(f32[2,1,72,1152]{3,2,1,0:T(8,128)} %slice.755, f32[2,1,72,3]{3,2,1,0:T(8,128)S(1)} %get-tuple-element.15, f32[2,1,72,3]{3,2,1,0:T(8,128)S(1)} %get-tuple-element.14, f32[2,1,72,1158]{3,2,1,0:T(8,128)S(1)} %concatenate.288), kind=kLoop, calls=%fused_computation.29 | loop fusion | flops 1829520 | bytes 2662848 | tf_op jit(solution)/shard_map/jit(clip)/min | solution.py:31
  56.7 0.7 fusion.13
  58.2 0.7 copy-done.10
  60.3 0.6 fusion.25
  62.2 0.7 fusion.4
  63.7 0.7 copy-done.16
  74.9 0.7 copy-done.24
  76.6 1.1 copy.245
  77.8 2.9 %reshape.765 = f32[16,1,6912]{2,1,0:T(1,128)} reshape(f32[1152,1,2,48]{3,2,1,0:T(2,128)S(1)} %bitcast.111) | data formatting | bytes 884736
  80.6 6.6 %all-to-all-start = ((f32[16,1,6912]{2,1,0:T(1,128)}), f32[16,1,6912]{2,1,0:T(1,128)S(1)}, u32[]{:S(2)}, u32[]{:S(2)}) async-start(f32[16,1,6912]{2,1,0:T(1,128)} %reshape.765), calls=%async_computation | async-start | bytes 884736 | tf_op jit(solution)/shard_map/all_to_all | solution.py:145
  87.6 0.9 pad_maximum_fusion.12
  88.5 0.7 copy.259
  89.7 2.7 %reduce.2 = f32[16,6912]{1,0:T(8,128)S(1)} reduce(f32[16,1,6912]{2,1,0:T(1,128)} %all-to-all-done.1, f32[]{:T(128)} %broadcast.437), dimensions={1}, to_apply=%all_to_all.38.reduce_sub_computation | reduce | bytes 884740 | tf_op jit(solution)/shard_map/all_to_all | solution.py:146
  92.4 1.9 %reshape.764 = f32[1152,1,2,48]{3,2,1,0:T(2,128)S(1)} reshape(f32[16,6912]{1,0:T(8,128)S(1)} %reduce.2) | data formatting | bytes 884736
  95.2 3.2 %all-to-all-done = f32[16,1,6912]{2,1,0:T(1,128)S(1)} async-done(((f32[16,1,6912]{2,1,0:T(1,128)}), f32[16,1,6912]{2,1,0:T(1,128)S(1)}, u32[]{:S(2)}, u32[]{:S(2)}) %all-to-all-start) | async-done | bytes 442400 | tf_op jit(solution)/shard_map/all_to_all | solution.py:145
  98.4 1.7 %reduce.3 = f32[16,6912]{1,0:T(8,128)S(1)} reduce(f32[16,1,6912]{2,1,0:T(1,128)S(1)} %all-to-all-done, f32[]{:T(128)} %broadcast.437), dimensions={1}, to_apply=%all_to_all.35.reduce_sub_computation | reduce | bytes 884740 | tf_op jit(solution)/shard_map/all_to_all | solution.py:145
  100.1 1.9 %reshape.766 = f32[1152,1,2,48]{3,2,1,0:T(2,128)S(1)} reshape(f32[16,6912]{1,0:T(8,128)S(1)} %reduce.3) | data formatting | bytes 884736
  105.2 0.8 copy-done.5
  106.9 1.0 copy.249
  107.9 4.1 %all-to-all-start.2 = ((f32[2,16,48,72]{3,2,0,1:T(8,128)}), f32[2,16,48,72]{3,2,0,1:T(8,128)S(1)}, u32[]{:S(2)}, u32[]{:S(2)}) async-start(f32[2,16,48,72]{3,2,0,1:T(8,128)} %copy.249), calls=%async_computation.2 | async-start | bytes 1572864 | tf_op jit(solution)/shard_map/all_to_all | solution.py:106
  111.9 0.7 fusion.147
  112.7 1.5 %abs_multiply_fusion.4 = (f32[49,1152]{1,0:T(8,128)}, f32[49,1152]{1,0:T(8,128)}) fusion(f32[48,1152]{1,0:T(8,128)S(1)} %fusion.165, f32[1,1152]{1,0:T(1,128)} %bitcast.41), kind=kLoop, calls=%fused_computation.260 | loop fusion | flops 282240 | bytes 677376 | tf_op jit(solution)/shard_map/mul | solution.py:55
  114.2 12.9 %all-to-all-done.2 = f32[2,16,48,72]{3,2,0,1:T(8,128)S(1)} async-done(((f32[2,16,48,72]{3,2,0,1:T(8,128)}), f32[2,16,48,72]{3,2,0,1:T(8,128)S(1)}, u32[]{:S(2)}, u32[]{:S(2)}) %all-to-all-start.2) | async-done | bytes 442400 | tf_op jit(solution)/shard_map/all_to_all | solution.py:106
  130.6 2.5 %collective-permute-start.3 = (f32[2,1,3,1152]{3,2,1,0:T(4,128)S(1)}, f32[2,1,3,1152]{3,2,1,0:T(4,128)S(1)}, u32[]{:S(2)}, u32[]{:S(2)}) collective-permute-start(f32[2,1,3,1152]{3,2,1,0:T(4,128)S(1)} %get-tuple-element.46), channel_id=1, source_target_pairs={{0,16},{16,32},{32,48},{48,64},{64,80},{80,96},{96,112},{112,128},... | collective-permute-start | bytes 82952 | tf_op jit(solution)/shard_map/ppermute | solution.py:21
  133.1 3.3 %collective-permute-start.4 = (f32[2,1,3,1152]{3,2,1,0:T(4,128)S(1)}, f32[2,1,3,1152]{3,2,1,0:T(4,128)S(1)}, u32[]{:S(2)}, u32[]{:S(2)}) collective-permute-start(f32[2,1,3,1152]{3,2,1,0:T(4,128)S(1)} %get-tuple-element.47), channel_id=1, source_target_pairs={{16,0},{32,16},{48,32},{64,48},{80,64},{96,80},{112,96},{128,112},... | collective-permute-start | bytes 82952 | tf_op jit(solution)/shard_map/ppermute | solution.py:24
  136.5 1.4 fusion.150
  137.8 0.7 reshape.761
  138.6 2.6 %collective-permute-done.4 = f32[2,1,3,1152]{3,2,1,0:T(4,128)S(1)} collective-permute-done((f32[2,1,3,1152]{3,2,1,0:T(4,128)S(1)}, f32[2,1,3,1152]{3,2,1,0:T(4,128)S(1)}, u32[]{:S(2)}, u32[]{:S(2)}) %collective-permute-start.4) | collective-permute-done | bytes 27680 | tf_op jit(solution)/shard_map/ppermute | solution.py:24
  141.6 0.8 copy-done.22
  143.0 0.8 fusion.140
  (188 shorter events, 30.2 us)
Async XLA Ops:
  0.6 10.4 %copy-start.37 = (f32[2,1,48,1152]{3,2,1,0:T(8,128)S(1)}, f32[2,1,48,1152]{3,2,1,0:T(8,128)}, u32[]{:S(2)}) copy-start(f32[2,1,48,1152]{3,2,1,0:T(8,128)} %param.7) | copy-start | bytes 1327108
  4.2 28.4 %collective-permute-start = (f32[4,1,12,1152]{3,2,1,0:T(8,128)}, f32[4,1,12,1152]{3,2,1,0:T(8,128)S(1)}, u32[]{:S(2)}, u32[]{:S(2)}) collective-permute-start(f32[4,1,12,1152]{3,2,1,0:T(8,128)} %get-tuple-element.18), channel_id=1, source_target_pairs={{0,16},{16,32},{32,48},{48,64},{64,80},{80,96},{96,112},{112,128},... | collective-permute-start | bytes 663560 | tf_op jit(solution)/shard_map/ppermute | solution.py:21
  9.1 23.5 %collective-permute-start.1 = (f32[4,1,12,1152]{3,2,1,0:T(8,128)}, f32[4,1,12,1152]{3,2,1,0:T(8,128)S(1)}, u32[]{:S(2)}, u32[]{:S(2)}) collective-permute-start(f32[4,1,12,1152]{3,2,1,0:T(8,128)} %get-tuple-element.19), channel_id=1, source_target_pairs={{16,0},{32,16},{48,32},{64,48},{80,64},{96,80},{112,96},{128,112},... | collective-permute-start | bytes 663560 | tf_op jit(solution)/shard_map/ppermute | solution.py:24
  12.1 9.4 %copy-start.2 = (f32[1,48,1152]{2,1,0:T(8,128)S(1)}, f32[1,48,1152]{2,1,0:T(8,128)}, u32[]{:S(2)}) copy-start(f32[1,48,1152]{2,1,0:T(8,128)} %param.6) | copy-start | bytes 663556
  12.2 16.9 %copy-start = (f32[1,48,1152]{2,1,0:T(8,128)S(1)}, f32[1,48,1152]{2,1,0:T(8,128)}, u32[]{:S(2)}) copy-start(f32[1,48,1152]{2,1,0:T(8,128)} %param.5) | copy-start | bytes 663556
  15.0 65.6 %all-to-all-start.1 = ((f32[16,1,6912]{2,1,0:T(1,128)}), f32[16,1,6912]{2,1,0:T(1,128)}, u32[]{:S(2)}, u32[]{:S(2)}) async-start(f32[16,1,6912]{2,1,0:T(1,128)} %reshape.763), calls=%async_computation.1 | async-start | bytes 884736 | tf_op jit(solution)/shard_map/all_to_all | solution.py:146
  21.5 11.1 %copy-start.1 = (f32[2,1,48,1152]{3,2,1,0:T(8,128)S(1)}, f32[2,1,48,1152]{3,2,1,0:T(8,128)}, u32[]{:S(2)}) copy-start(f32[2,1,48,1152]{3,2,1,0:T(8,128)} %param.4) | copy-start | bytes 1327108
  21.6 11.0 %copy-start.35 = (f32[1,48,1152]{2,1,0:T(8,128)}, f32[1,48,1152]{2,1,0:T(8,128)S(1)}, u32[]{:S(2)}) copy-start(f32[1,48,1152]{2,1,0:T(8,128)S(1)} %broadcast_select_fusion) | copy-start | bytes 663556
  22.2 65.4 %collective-permute-start.2 = (f32[1,1,1152]{2,1,0:T(1,128)}, f32[1,1,1152]{2,1,0:T(1,128)}, u32[]{:S(2)}, u32[]{:S(2)}) collective-permute-start(f32[1,1,1152]{2,1,0:T(1,128)} %slice.902), channel_id=1, source_target_pairs={{0,16},{16,32},{32,48},{48,64},{64,80},{80,96},{96,112},{112,128},... | collective-permute-start | bytes 13832 | tf_op jit(solution)/shard_map/ppermute | solution.py:13
  55.5 0.8 copy-start.47
  55.5 1.0 copy-start.8
  55.6 1.1 copy-start.9
  55.6 1.1 copy-start.39
  58.0 1.0 copy-start.10
  58.0 1.1 copy-start.11
  58.0 1.2 copy-start.12
  58.0 1.2 copy-start.40
  59.1 0.6 copy-start.51
  61.0 1.0 copy-start.13
  61.0 1.0 copy-start.46
  61.0 1.1 copy-start.6
  61.0 1.2 copy-start.7
  61.0 1.2 copy-start.38
  63.5 1.0 copy-start.16
  63.5 1.0 copy-start.17
  63.5 1.1 copy-start.18
  63.5 1.1 copy-start.42
  64.6 0.6 copy-start.50
  66.4 1.0 copy-start.19
  66.4 1.0 copy-start.48
  66.4 1.1 copy-start.14
  66.4 1.2 copy-start.15
  66.5 1.2 copy-start.41
  68.8 0.9 copy-start.28
  68.8 1.1 copy-start.29
  68.8 1.2 copy-start.30
  68.8 1.2 copy-start.45
  70.0 0.7 copy-start.49
  71.7 0.9 copy-start.27
  72.1 1.5 %copy-start.20 = (f32[54,1153]{1,0:T(8,128)S(1)}, f32[54,1153]{1,0:T(8,128)}, u32[]{:S(2)}) copy-start(f32[54,1153]{1,0:T(8,128)} %get-tuple-element.82) | copy-start | bytes 747148
  72.1 1.5 %copy-start.21 = (f32[54,1153]{1,0:T(8,128)S(1)}, f32[54,1153]{1,0:T(8,128)}, u32[]{:S(2)}) copy-start(f32[54,1153]{1,0:T(8,128)} %get-tuple-element.83) | copy-start | bytes 747148
  72.1 1.5 %copy-start.43 = (pred[54,1153]{1,0:T(8,128)(4,1)S(1)}, pred[54,1153]{1,0:T(8,128)(4,1)}, u32[]{:S(2)}) copy-start(pred[54,1153]{1,0:T(8,128)(4,1)} %fusion.148) | copy-start | bytes 186790
  74.7 0.9 copy-start.24
  74.7 1.1 copy-start.25
  74.7 1.2 copy-start.26
  74.7 1.2 copy-start.44
  75.9 0.6 copy-start.52
  77.8 9.6 %copy-start.36 = (f32[1,48,1152]{2,1,0:T(8,128)S(1)}, f32[1,48,1152]{2,1,0:T(8,128)}, u32[]{:S(2)}) copy-start(f32[1,48,1152]{2,1,0:T(8,128)} %copy-done.35) | copy-start | bytes 663556
  80.6 17.7 %all-to-all-start = ((f32[16,1,6912]{2,1,0:T(1,128)}), f32[16,1,6912]{2,1,0:T(1,128)S(1)}, u32[]{:S(2)}, u32[]{:S(2)}) async-start(f32[16,1,6912]{2,1,0:T(1,128)} %reshape.765), calls=%async_computation | async-start | bytes 884736 | tf_op jit(solution)/shard_map/all_to_all | solution.py:145
  103.2 0.8 copy-start.3
  104.2 0.8 copy-start.4
  105.2 0.8 copy-start.5
  107.9 19.2 %all-to-all-start.2 = ((f32[2,16,48,72]{3,2,0,1:T(8,128)}), f32[2,16,48,72]{3,2,0,1:T(8,128)S(1)}, u32[]{:S(2)}, u32[]{:S(2)}) async-start(f32[2,16,48,72]{3,2,0,1:T(8,128)} %copy.249), calls=%async_computation.2 | async-start | bytes 1572864 | tf_op jit(solution)/shard_map/all_to_all | solution.py:106
  128.7 0.9 copy-start.32
  128.7 1.1 copy-start.33
  128.7 1.2 copy-start.34
  130.6 7.9 %collective-permute-start.3 = (f32[2,1,3,1152]{3,2,1,0:T(4,128)S(1)}, f32[2,1,3,1152]{3,2,1,0:T(4,128)S(1)}, u32[]{:S(2)}, u32[]{:S(2)}) collective-permute-start(f32[2,1,3,1152]{3,2,1,0:T(4,128)S(1)} %get-tuple-element.46), channel_id=1, source_target_pairs={{0,16},{16,32},{32,48},{48,64},{64,80},{80,96},{96,112},{112,128},... | collective-permute-start | bytes 82952 | tf_op jit(solution)/shard_map/ppermute | solution.py:21
  133.1 8.0 %collective-permute-start.4 = (f32[2,1,3,1152]{3,2,1,0:T(4,128)S(1)}, f32[2,1,3,1152]{3,2,1,0:T(4,128)S(1)}, u32[]{:S(2)}, u32[]{:S(2)}) collective-permute-start(f32[2,1,3,1152]{3,2,1,0:T(4,128)S(1)} %get-tuple-element.47), channel_id=1, source_target_pairs={{16,0},{32,16},{48,32},{64,48},{80,64},{96,80},{112,96},{128,112},... | collective-permute-start | bytes 82952 | tf_op jit(solution)/shard_map/ppermute | solution.py:24
  141.4 0.9 copy-start.22
  141.4 1.1 copy-start.23
  141.5 1.2 copy-start.31
where the time goes:
time: 145 us; the launch traced here: 144 us
  other arithmetic  49.1 us (34%)
  local copies, waits for them, and re-layouts  37.9 us (26%)
  starting transfers between devices  36.6 us (25%)
  waiting for transfers between devices  18.6 us (13%)
  between operations  1.66 us (1%)
    unnamed x113, local copies, waits for them, and re-layouts  21.7 us
    all_to_all x1, waiting for transfers between devices, columns_settle(): lax.all_to_all(settled.reshape(shape_full), 'lev', split_axis=1, concat_a...  12.9 us
    mul x18, other arithmetic, sweep(): face_flux_values = courant * jnp.where(courant >= 0, from_west, from_east)  9.92 us
    ppermute x2, starting transfers between devices, extended_2(): lax.ppermute(lax.slice_in_dim(block, block.shape[dim] - width, None, axis...  7.44 us
    ppermute x1, starting transfers between devices, passed_along(): return lax.ppermute(block, axis, route)  6.81 us
    ge x10, other arithmetic, sweep(): face_flux_values = courant * jnp.where(courant >= 0, from_west, from_east)  6.78 us
    all_to_all x1, starting transfers between devices, on_device(): lax.all_to_all(field, 'lev', split_axis=3, concat_axis=1, tiled=True)  6.57 us
    mul x6, other arithmetic, sweep(): 0.5 * courant_abs  6.5 us
  transfers between devices with their start and end apart: 8, of which 3 were waited for; matrix products, arithmetic and copies ran while one was open for 42% of the time, Pallas kernels for 0%

commit v1 on v0

v1 whole, which is shorter than its diff:
```python
import functools

import jax
import jax.numpy as jnp
from jax import lax
from jax.experimental import pallas as pl
from jax.experimental.pallas import tpu as pltpu
from jax.sharding import PartitionSpec as P

HSUB = 4
SETTLE_SUBSTEPS = 6
SUB = 8
LANE = 128
MESH = pl.DeviceIdType.MESH
VMEM = pltpu.VMEM
DMA = pltpu.SemaphoreType.DMA


def coefficients(k):
    s = jnp.abs(k)
    half = 0.5 * k * s
    a3 = 3.0 * half * (1.0 - (2.0 / 3.0) * s)
    return k - a3 - half, 2.0 * a3, half - a3


def face_value(a, b, c, d):
    value = (7.0 / 12.0) * (b + c) - (1.0 / 12.0) * (a + d)
    return jnp.minimum(jnp.maximum(value, jnp.minimum(b, c)), jnp.maximum(b, c))


def row_of(ref, index, tiles):
    return jnp.concatenate([ref[index + v] for v in range(tiles)], axis=1)


def kernel(
    bands, levels,
    tracer, east, north, fall, out, deposit,
    flat, q, z, q2, cz, cm, hs, hr, ns, nr, fs, rf, rw, so, dp, dr,
    in_sem, out_sem, hs_sem, hr_sem, n_sem, fs_sem, fr_sem, ws_sem, wr_sem, bs_sem, br_sem, ds_sem, dr_sem,
):
    bins, rows, width = tracer.shape
    tall = rows // SUB
    wide = width // LANE
    groups = bins * tall
    tiles = groups * wide
    share = so.shape[1]
    chunk = deposit.shape[2]
    band = lax.axis_index("lat")
    me = lax.axis_index("lev")
    has_south, has_north = band > 0, band < bands - 1
    sub = lax.broadcasted_iota(jnp.int32, (SUB, LANE), 0)
    first, last = sub == 0, sub == SUB - 1

    def peer(k):
        return lax.rem(me + k, levels)

    barrier = pltpu.get_barrier_semaphore()
    for k in range(1, levels):
        pl.semaphore_signal(barrier, inc=1, device_id={"lev": peer(k)}, device_id_type=MESH)

    @pl.when(has_south)
    def _():
        pl.semaphore_signal(barrier, inc=1, device_id={"lat": band - 1}, device_id_type=MESH)

    @pl.when(has_north)
    def _():
        pl.semaphore_signal(barrier, inc=1, device_id={"lat": band + 1}, device_id_type=MESH)

    def fetch(source, slot):
        return [
            pltpu.make_async_copy(
                source.at[:, pl.ds(v * LANE, LANE)], flat.at[slot, v], in_sem.at[slot, v]
            )
            for v in range(wide)
        ]

    fetched = [fetch(north, 0), fetch(east, 1)]
    fetched += [fetch(tracer.at[b], 2 + b) for b in range(bins)]
    fetched += [fetch(fall.at[b], 2 + bins + b) for b in range(bins)]
    for copies in fetched:
        for copy in copies:
            copy.start()
    for copies in fetched:
        for copy in copies:
            copy.wait()

    for j in range(tall):
        for v in range(wide):
            picked = pl.ds(j, SUB, stride=tall)
            k = flat[0, v, picked, :]
            if j == tall - 1:
                k = jnp.where(jnp.logical_and(last, band == bands - 1), 0.0, k)
                ns[v : v + 1, :] = k[SUB - 1 :, :]
            cm[3, j + 1, v] = k
            for i, c in enumerate(coefficients(flat[1, v, picked, :])):
                cz[i, j, v] = c
            for b in range(bins):
                index = (b * tall + j) * wide + v
                q[index] = flat[2 + b, v, picked, :]
                fs[index] = flat[2 + bins + b, v, picked, :]
    for index in range(tiles, q.shape[0]):
        q[index] = jnp.zeros((SUB, LANE), jnp.float32)
        fs[index] = jnp.zeros((SUB, LANE), jnp.float32)

    @pl.when(band == 0)
    def _():
        nr[...] = jnp.zeros_like(nr)
        for s in range(HSUB + 1):
            for b in range(bins):
                hr[s, 0, b] = jnp.zeros(hr.shape[3:], jnp.float32)

    @pl.when(band == bands - 1)
    def _():
        for s in range(HSUB + 1):
            for b in range(bins):
                hr[s, 1, b] = jnp.zeros(hr.shape[3:], jnp.float32)

    pl.semaphore_wait(barrier, levels - 1 + has_south.astype(jnp.int32) + has_north.astype(jnp.int32))

    north_row = pltpu.make_async_remote_copy(
        ns, nr, n_sem.at[0], n_sem.at[1], device_id={"lat": band + 1}, device_id_type=MESH
    )

    @pl.when(has_north)
    def _():
        north_row.start()

    def halo(s, side, b):
        target = band + 1 if side == 0 else band - 1
        return pltpu.make_async_remote_copy(
            hs.at[s, side, b], hr.at[s, side, b], hs_sem.at[s, side, b], hr_sem.at[s, side, b],
            device_id={"lat": target}, device_id_type=MESH,
        )

    def deal(source, target, send_sem, recv_sem, k):
        return pltpu.make_async_remote_copy(
            source.at[pl.ds(peer(k) * share, share)], target.at[me], send_sem.at[k], recv_sem.at[me],
            device_id={"lev": peer(k)}, device_id_type=MESH,
        )

    def dealt(source, target, send_sem, recv_sem, k):
        return pltpu.make_async_remote_copy(
            source.at[pl.ds(me * share, share)], target.at[peer(k)], send_sem.at[k], recv_sem.at[peer(k)],
            device_id={"lev": peer(k)}, device_id_type=MESH,
        )

    def zonal(s, b, field):
        for j in range(tall):
            base = (b * tall + j) * wide
            mid = row_of(field, base, wide)
            west = pltpu.roll(mid, 1, 1)
            east_1 = pltpu.roll(mid, width - 1, 1)
            east_2 = pltpu.roll(mid, width - 2, 1)
            face = face_value(west, mid, east_1, east_2)
            c0 = jnp.concatenate([cz[0, j, v] for v in range(wide)], axis=1)
            c1 = jnp.concatenate([cz[1, j, v] for v in range(wide)], axis=1)
            c2 = jnp.concatenate([cz[2, j, v] for v in range(wide)], axis=1)
            up = c1 >= 0
            flux = (
                c0 * face
                + c1 * jnp.where(up, mid, east_1)
                + c2 * jnp.where(up, pltpu.roll(face, 1, 1), pltpu.roll(face, width - 1, 1))
            )
            new = mid - (flux - pltpu.roll(flux, 1, 1))
            for v in range(wide):
                z[base + v] = new[:, v * LANE : (v + 1) * LANE]
                if j < 3:
                    hs[s, 1, b, pl.ds(j * wide + v, 1), :] = new[:1, v * LANE : (v + 1) * LANE]
                if j >= tall - 3:
                    hs[s, 0, b, pl.ds((j - tall + 3) * wide + v, 1), :] = new[SUB - 1 :, v * LANE : (v + 1) * LANE]

        @pl.when(has_north)
        def _():
            halo(s, 0, b).start()

        @pl.when(has_south)
        def _():
            halo(s, 1, b).start()

    def meridional(s, b, store):
        @pl.when(has_south)
        def _():
            halo(s, 0, b).wait_recv()

        @pl.when(has_north)
        def _():
            halo(s, 1, b).wait_recv()

        for v in range(wide):
            own = [z[(b * tall + j) * wide + v] for j in range(tall)]
            below = [
                jnp.where(first, hr[s, 0, b, pl.ds(i * wide + v, 1), :], pltpu.roll(own[tall - 3 + i], 1, 0))
                for i in range(3)
            ]
            above = [
                jnp.where(last, hr[s, 1, b, pl.ds(i * wide + v, 1), :], pltpu.roll(own[i], SUB - 1, 0))
                for i in range(3)
            ]
            ext = jnp.stack(below + own + above)
            face = face_value(ext[: tall + 3], ext[1 : tall + 4], ext[2 : tall + 5], ext[3:])
            c0, c1, c2 = cm[0, :, v], cm[1, :, v], cm[2, :, v]
            up = c1 >= 0
            flux = (
                c0 * face[1 : tall + 2]
                + c1 * jnp.where(up, ext[2 : tall + 3], ext[3 : tall + 4])
                + c2 * jnp.where(up, face[: tall + 1], face[2:])
            )
            new = ext[3 : tall + 3] - (flux[1:] - flux[:-1])
            for j in range(tall):
                store(b, j, v, new[j])

    def keep(b, j, v, tile):
        q[(b * tall + j) * wide + v] = tile

    def finish(b, j, v, tile):
        flat[b, v, pl.ds(j, SUB, stride=tall), :] = tile

    per_step = -(-levels // HSUB)

    def substep(s, carry):
        for b in range(bins):
            zonal(s, b, q)
        for i in range(per_step):
            k = s * per_step + i

            @pl.when(jnp.logical_and(k > 0, k < levels))
            def _():
                deal(fs, rf, fs_sem, fr_sem, k).start()

        @pl.when(s == 0)
        def _():
            @pl.when(has_south)
            def _():
                north_row.wait_recv()

            for v in range(wide):
                low = jnp.where(first, nr[v : v + 1, :], pltpu.roll(cm[3, tall, v], 1, 0))
                for j in range(tall + 1):
                    for i, c in enumerate(coefficients(cm[3, j, v] if j else low)):
                        cm[i, j, v] = c

        for b in range(bins):
            meridional(s, b, keep)
        return carry

    lax.fori_loop(0, HSUB, substep, 0)

    for k in range(1, levels):
        deal(q, rw, ws_sem, wr_sem, k).start()
    for i in range(share):
        rw[me, i] = q[me * share + i]
        rf[me, i] = fs[me * share + i]
    for k in range(1, levels):
        dealt(fs, rf, fs_sem, fr_sem, k).wait_recv()
    for k in range(1, levels):
        dealt(q, rw, ws_sem, wr_sem, k).wait_recv()

    def settle(i, carry):
        mass = rw[:, i]
        half = 0.5 * rf[:, i]
        fallen = jnp.zeros((SUB, LANE), jnp.float32)
        for _ in range(SETTLE_SUBSTEPS):
            flux = (mass * half) * (2.0 + jnp.tanh(mass))
            inflow = jnp.concatenate([jnp.zeros((1, SUB, LANE), jnp.float32), flux[:-1]], axis=0)
            mass = (mass + inflow) - flux
            fallen = fallen + flux[levels - 1]
        so[:, i] = mass
        dp[i] = fallen
        return carry

    lax.fori_loop(0, share, settle, 0)

    def give_back(k):
        return pltpu.make_async_remote_copy(
            so.at[peer(k)], q2.at[pl.ds(me * share, share)], bs_sem.at[k], br_sem.at[me],
            device_id={"lev": peer(k)}, device_id_type=MESH,
        )

    def given_back(k):
        return pltpu.make_async_remote_copy(
            so.at[peer(k)], q2.at[pl.ds(peer(k) * share, share)], bs_sem.at[k], br_sem.at[peer(k)],
            device_id={"lev": peer(k)}, device_id_type=MESH,
        )

    for k in range(1, levels):
        give_back(k).start()
    for i in range(share):
        q2[me * share + i] = so[me, i]

    reach = max((LANE * v + LANE - 1) // chunk - (LANE * v) // chunk for v in range(wide)) + 1

    def sent(i, e):
        tile = me * share + i
        v = lax.rem(tile, wide)
        target = (LANE * v) // chunk + e
        valid = jnp.logical_and(tile < tiles, target <= (LANE * v + LANE - 1) // chunk)
        slot = (tile // wide) * 2 + v - (chunk * target) // LANE
        return target, valid, slot

    def drop(i, e):
        target, valid, slot = sent(i, e)
        away = jnp.logical_and(valid, target != me)
        copy = pltpu.make_async_remote_copy(
            dp.at[i], dr.at[slot], ds_sem.at[i, e], dr_sem.at[slot],
            device_id={"lev": target}, device_id_type=MESH,
        )
        return copy, away

    for i in range(share):
        for e in range(reach):
            copy, away = drop(i, e)
            target, valid, slot = sent(i, e)

            @pl.when(away)
            def _():
                copy.start()

            @pl.when(jnp.logical_and(valid, target == me))
            def _():
                dr[slot] = dp[i]

    for k in range(1, levels):
        given_back(k).wait_recv()

    for b in range(bins):
        zonal(HSUB, b, q2)
    written = [
        [
            pltpu.make_async_copy(
                flat.at[b, v], out.at[b, :, pl.ds(v * LANE, LANE)], out_sem.at[b, v]
            )
            for v in range(wide)
        ]
        for b in range(bins)
    ]
    for b in range(bins):
        meridional(HSUB, b, finish)
        for copy in written[b]:
            copy.start()

    low_tile = (chunk * me) // LANE
    high_tile = (chunk * me + chunk - 1) // LANE
    offset = chunk * me - LANE * low_tile
    for g in range(groups):
        for e in range(2):
            slot = 2 * g + e
            tile = g * wide + low_tile + e
            used = low_tile + e <= high_tile
            source = tile // share

            @pl.when(jnp.logical_and(used, source != me))
            def _():
                pltpu.make_async_remote_copy(
                    dp.at[0], dr.at[slot], ds_sem.at[0, 0], dr_sem.at[slot],
                    device_id={"lev": lax.rem(me + 1, levels)}, device_id_type=MESH,
                ).wait_recv()

            @pl.when(jnp.logical_not(used))
            def _():
                dr[slot] = jnp.zeros((SUB, LANE), jnp.float32)

        both = jnp.concatenate([dr[2 * g], dr[2 * g + 1]], axis=1)
        both = pltpu.roll(both, lax.rem(2 * LANE - offset, 2 * LANE), 1)
        flat[bins + g // tall, 0, pl.ds(g % tall, SUB, stride=tall), :] = both[:, :LANE]
    for b in range(bins):
        deposit[b] = flat[bins + b, 0][:, :chunk]
    for copies in written:
        for copy in copies:
            copy.wait()

    @pl.when(has_north)
    def _():
        north_row.wait_send()

    for s in range(HSUB + 1):
        for b in range(bins):
            @pl.when(has_north)
            def _():
                halo(s, 0, b).wait_send()

            @pl.when(has_south)
            def _():
                halo(s, 1, b).wait_send()

    for k in range(1, levels):
        deal(fs, rf, fs_sem, fr_sem, k).wait_send()
        deal(q, rw, ws_sem, wr_sem, k).wait_send()
        give_back(k).wait_send()
    for i in range(share):
        for e in range(reach):
            copy, away = drop(i, e)

            @pl.when(away)
            def _():
                copy.wait_send()


def on_device(bands, levels, tracer, east, north, fall):
    bins, _, rows, width = tracer.shape
    tall, wide = rows // SUB, width // LANE
    tiles = bins * tall * wide
    share = -(-tiles // levels)
    chunk = width // levels
    reach = max((LANE * v + LANE - 1) // chunk - (LANE * v) // chunk for v in range(wide)) + 1
    edge = -(-3 * wide // SUB) * SUB
    line = -(-wide // SUB) * SUB
    steps = HSUB + 1
    f32 = jnp.float32
    out, deposit = pl.pallas_call(
        functools.partial(kernel, bands, levels),
        out_shape=(
            jax.ShapeDtypeStruct((bins, rows, width), f32),
            jax.ShapeDtypeStruct((bins, rows, chunk), f32),
        ),
        in_specs=[pl.BlockSpec(memory_space=pltpu.HBM)] * 4,
        out_specs=(pl.BlockSpec(memory_space=pltpu.HBM), pl.BlockSpec(memory_space=VMEM)),
        scratch_shapes=[
            VMEM((2 + 2 * bins, wide, rows, LANE), f32),
            VMEM((share * levels, SUB, LANE), f32),
            VMEM((tiles, SUB, LANE), f32),
            VMEM((share * levels, SUB, LANE), f32),
            VMEM((3, tall, wide, SUB, LANE), f32),
            VMEM((4, tall + 1, wide, SUB, LANE), f32),
            VMEM((steps, 2, bins, edge, LANE), f32),
            VMEM((steps, 2, bins, edge, LANE), f32),
            VMEM((line, LANE), f32),
            VMEM((line, LANE), f32),
            VMEM((share * levels, SUB, LANE), f32),
            VMEM((levels, share, SUB, LANE), f32),
            VMEM((levels, share, SUB, LANE), f32),
            VMEM((levels, share, SUB, LANE), f32),
            VMEM((share, SUB, LANE), f32),
            VMEM((2 * bins * tall, SUB, LANE), f32),
            DMA((2 + 2 * bins, wide)),
            DMA((bins, wide)),
            DMA((steps, 2, bins)),
            DMA((steps, 2, bins)),
            DMA((2,)),
            DMA((levels,)),
            DMA((levels,)),
            DMA((levels,)),
            DMA((levels,)),
            DMA((levels,)),
            DMA((levels,)),
            DMA((share, reach)),
            DMA((2 * bins * tall,)),
        ],
        compiler_params=pltpu.CompilerParams(
            collective_id=0, has_side_effects=True, vmem_limit_bytes=32 * 1024 * 1024
        ),
        cost_estimate=pl.CostEstimate(flops=50000000, bytes_accessed=3000000, transcendentals=700000),
    )(
        tracer.reshape(bins, rows, width),
        east.reshape(rows, width),
        north.reshape(rows, width),
        fall.reshape(bins, rows, width),
    )
    return out.reshape(tracer.shape), deposit


def solution(mesh):
    in_specs = (
        P(None, "lev", "lat", None),
        P("lev", "lat", None),
        P("lev", "lat", None),
        P(None, "lev", "lat", None),
    )
    out_specs = (P(None, "lev", "lat", None), P(None, "lat", "lev"))
    return jax.shard_map(
        functools.partial(on_device, mesh.shape["lat"], mesh.shape["lev"]),
        mesh=mesh, in_specs=in_specs, out_specs=out_specs, check_vma=False,
    )
```

time: 145 us -> 61.8 us (0.43)
  Pallas kernels: 0 us -> 55.1 us
  other arithmetic: 49.1 us -> 0 us
  starting transfers between devices: 36.6 us -> 0 us
  local copies, waits for them, and re-layouts: 37.9 us -> 5.27 us
  waiting for transfers between devices: 18.6 us -> 0 us
    pallas_call x0 -> x1, Pallas kernels: none -> 55.1 us  [on_device(): pl.pallas_call(functools.partial(kernel, bands, levels), out_shape=(jax.S...]
    ppermute x5 -> x0, starting transfers between devices: 19.5 us -> none  [the longest x2 7.44 us: extended_2(): lax.ppermute(lax.slice_in_dim(block, block.shape[dim] - width, None, axis...]
    mul x30 -> x0, other arithmetic: 17.9 us -> none  [the longest x18 9.92 us: sweep(): face_flux_values = courant * jnp.where(courant >= 0, from_west, from_east)]
    all_to_all x3 -> x0, starting transfers between devices: 17.1 us -> none  [the longest x1 6.57 us: on_device(): lax.all_to_all(field, 'lev', split_axis=3, concat_axis=1, tiled=True)]
    unnamed x113 -> x10, local copies, waits for them, and re-layouts: 21.7 us -> 5.27 us
    all_to_all x3 -> x0, waiting for transfers between devices: 16 us -> none  [the longest x1 12.9 us: columns_settle(): lax.all_to_all(settled.reshape(shape_full), 'lev', split_axis=1, concat_a...]
    ge x10 -> x0, other arithmetic: 6.78 us -> none  [sweep(): face_flux_values = courant * jnp.where(courant >= 0, from_west, from_east)]
    slice x17 -> x0, local copies, waits for them, and re-layouts: 6.58 us -> none  [the longest x14 5.07 us: window_for_cell(): return lax.slice_in_dim(source, start, start + length, axis=axis_dim)]
  transfers between devices with their start and end apart: 8 -> 0, of which waited for: 3 -> 0; matrix products, arithmetic and copies ran while one was open for 42% -> 0% of each run, Pallas kernels for 0% -> 0%
where the time goes in v1:
time: 61.8 us; the launch traced here: 61 us
  Pallas kernels  55.1 us (89%)
  local copies, waits for them, and re-layouts  5.27 us (9%)
  between operations  0.65 us (1%)
    pallas_call x1, Pallas kernels, on_device(): pl.pallas_call(functools.partial(kernel, bands, levels), out_shape=(jax.S...  55.1 us
    unnamed x10, local copies, waits for them, and re-layouts  5.27 us

profile of v1, /device:TPU:104, one launch (start us, length us, event | category | flops | bytes accessed | tf_op | source)
XLA Modules:
  0.0 61.0 jit_solution(11742861601412353975)
XLA Ops:
  0.6 0.0 copy-start
  0.6 1.0 %copy-done = f32[2,1,48,1152]{3,2,1,0:T(8,128)S(1)} copy-done((f32[2,1,48,1152]{3,2,1,0:T(8,128)S(1)}, f32[2,1,48,1152]{3,2,1,0:T(8,128)}, u32[]{:S(2)}) %copy-start) | copy-done | bytes 442392
  1.6 0.0 copy-start.1
  1.6 1.0 %copy-done.1 = f32[2,1,48,1152]{3,2,1,0:T(8,128)S(1)} copy-done((f32[2,1,48,1152]{3,2,1,0:T(8,128)S(1)}, f32[2,1,48,1152]{3,2,1,0:T(8,128)}, u32[]{:S(2)}) %copy-start.1) | copy-done | bytes 442392
  2.7 0.0 copy-start.2
  2.7 0.9 %copy-done.2 = f32[1,48,1152]{2,1,0:T(8,128)S(1)} copy-done((f32[1,48,1152]{2,1,0:T(8,128)S(1)}, f32[1,48,1152]{2,1,0:T(8,128)}, u32[]{:S(2)}) %copy-start.2) | copy-done | bytes 221208
  3.6 0.0 copy-start.3
  3.6 0.9 %copy-done.3 = f32[1,48,1152]{2,1,0:T(8,128)S(1)} copy-done((f32[1,48,1152]{2,1,0:T(8,128)S(1)}, f32[1,48,1152]{2,1,0:T(8,128)}, u32[]{:S(2)}) %copy-start.3) | copy-done | bytes 221208
  4.5 55.1 %shard_map.59 = (f32[2,48,1152]{2,1,0:T(8,128)S(1)}, f32[2,48,72]{2,1,0:T(8,128)S(1)}) custom-call(f32[2,48,1152]{2,1,0:T(8,128)S(1)} %bitcast.8, f32[48,1152]{1,0:T(8,128)S(1)} %bitcast.10, f32[48,1152]{1,0:T(8,128)S(1)} %bitcast.11, f32[2,48,1152]{2,1,0:T(8,128)S(1)} %bitcast.9), custom_call_target="tpu_custom_call" | custom-call | flops 50000000 | bytes 3000000 | tf_op jit(solution)/shard_map/pallas_call | solution.py:409
  59.6 0.8 %copy.9 = f32[2,1,48,1152]{3,2,1,0:T(8,128)} copy(f32[2,1,48,1152]{3,2,1,0:T(8,128)S(1)} %bitcast.7) | data formatting | bytes 884736
  60.4 0.6 %copy.10 = f32[2,48,72]{2,1,0:T(8,128)} copy(f32[2,48,72]{2,1,0:T(8,128)S(1)} %get-tuple-element.11) | data formatting | bytes 55296
Async XLA Ops:
  0.6 1.0 %copy-start = (f32[2,1,48,1152]{3,2,1,0:T(8,128)S(1)}, f32[2,1,48,1152]{3,2,1,0:T(8,128)}, u32[]{:S(2)}) copy-start(f32[2,1,48,1152]{3,2,1,0:T(8,128)} %param.4) | copy-start | bytes 1327108
  1.6 1.0 %copy-start.1 = (f32[2,1,48,1152]{3,2,1,0:T(8,128)S(1)}, f32[2,1,48,1152]{3,2,1,0:T(8,128)}, u32[]{:S(2)}) copy-start(f32[2,1,48,1152]{3,2,1,0:T(8,128)} %param.7) | copy-start | bytes 1327108
  2.7 0.9 %copy-start.2 = (f32[1,48,1152]{2,1,0:T(8,128)S(1)}, f32[1,48,1152]{2,1,0:T(8,128)}, u32[]{:S(2)}) copy-start(f32[1,48,1152]{2,1,0:T(8,128)} %param.5) | copy-start | bytes 663556
  3.6 0.9 %copy-start.3 = (f32[1,48,1152]{2,1,0:T(8,128)S(1)}, f32[1,48,1152]{2,1,0:T(8,128)}, u32[]{:S(2)}) copy-start(f32[1,48,1152]{2,1,0:T(8,128)} %param.6) | copy-start | bytes 663556

commit v2 on v0

v2 whole, which is shorter than its diff:
```python
import functools

import jax
import jax.numpy as jnp
from jax import lax
from jax.experimental import pallas as pl
from jax.experimental.pallas import tpu as pltpu
from jax.sharding import PartitionSpec as P

HSUB = 4
SETTLE_SUBSTEPS = 6
SUB = 8
LANE = 128
MESH = pl.DeviceIdType.MESH
VMEM = pltpu.VMEM
DMA = pltpu.SemaphoreType.DMA
scope = jax.named_scope


def coefficients(k):
    s = jnp.abs(k)
    half = 0.5 * k * s
    a3 = 3.0 * half * (1.0 - (2.0 / 3.0) * s)
    return k - a3 - half, 2.0 * a3, half - a3


def swept(ext, c0, c1, c2):
    n = ext.shape[0] - 6
    b, c = ext[1 : n + 4], ext[2 : n + 5]
    face = (7.0 / 12.0) * (b + c) - (1.0 / 12.0) * (ext[: n + 3] + ext[3:])
    face = jnp.minimum(jnp.maximum(face, jnp.minimum(b, c)), jnp.maximum(b, c))
    up = c1 >= 0
    flux = (
        c0 * face[1 : n + 2]
        + c1 * jnp.where(up, ext[2 : n + 3], ext[3 : n + 4])
        + c2 * jnp.where(up, face[: n + 1], face[2:])
    )
    return ext[3 : n + 3] - (flux[1:] - flux[:-1])


def kernel(
    bands, levels,
    tracer, east, north, fall, out, deposit,
    flat, turn, q, z, q2, q3, fs, cz, cm, hs, hr, ns, nr, rf, rw, so, dblk, dts, dr,
    in_sem, out_sem, hs_sem, hr_sem, n_sem, f_sem, w_sem, b_sem, d_sem,
):
    bins, rows, width = tracer.shape
    tall = rows // SUB
    wide = width // LANE
    main = tall * (wide - 1) // levels
    each = main + 1
    spare = 1 if bins * tall <= levels else bins
    share = main * bins + spare
    across = levels // 4
    lanes_each = LANE // levels
    chunk = width // levels
    groups = [(b, j) for b in range(bins) for j in range(tall)]
    band = lax.axis_index("lat")
    me = lax.axis_index("lev")
    has_south, has_north = band > 0, band < bands - 1
    sub = lax.broadcasted_iota(jnp.int32, (SUB, LANE), 0)
    first, last = sub == 0, sub == SUB - 1

    half_at, x_at, core_at = me // (2 * across), lax.rem(me // 2, across), lax.rem(me, 2)
    moves = [
        (h, x, c)
        for h in (1, 0)
        for x in sorted(range(across), key=lambda x: -min(x, across - x))
        for c in range(2)
        if (h, x, c) != (0, 0, 0)
    ]
    n_moves = len(moves)
    same_half = [i for i, m in enumerate(moves) if m[0] == 0]
    other_half = [i for i, m in enumerate(moves) if m[0] == 1]

    def at(h, x, c):
        return (lax.rem(half_at + h, 2) * across + lax.rem(x_at + x, across)) * 2 + lax.rem(core_at + c, 2)

    def to(i):
        return at(*moves[i])

    def origin(i):
        h, x, c = moves[i]
        return at(h, across - x, c)

    barrier = pltpu.get_barrier_semaphore()
    for i in range(n_moves):
        pl.semaphore_signal(barrier, inc=1, device_id={"lev": to(i)}, device_id_type=MESH)

    @pl.when(has_south)
    def _():
        pl.semaphore_signal(barrier, inc=1, device_id={"lat": band - 1}, device_id_type=MESH)

    @pl.when(has_north)
    def _():
        pl.semaphore_signal(barrier, inc=1, device_id={"lat": band + 1}, device_id_type=MESH)

    def fetch(source, slot):
        return [
            pltpu.make_async_copy(
                source.at[:, pl.ds(v * LANE, LANE)], flat.at[slot, v], in_sem.at[slot]
            )
            for v in range(wide)
        ]

    fetched = [fetch(tracer.at[b], b) for b in range(bins)] + [fetch(east, bins), fetch(north, bins + 1)]
    fetched += [fetch(fall.at[b], bins + 2 + b) for b in range(bins)]
    for copies in fetched:
        for copy in copies:
            copy.start()

    @pl.when(band == 0)
    def _():
        nr[...] = jnp.zeros_like(nr)
        for s in range(HSUB + 1):
            for b in range(bins):
                hr[0, s, b] = jnp.zeros(hr.shape[3:], jnp.float32)

    @pl.when(band == bands - 1)
    def _():
        for s in range(HSUB + 1):
            for b in range(bins):
                hr[1, s, b] = jnp.zeros(hr.shape[3:], jnp.float32)

    dblk[...] = jnp.zeros_like(dblk)

    def spread(slot, emit):
        for i in range(2):
            pltpu.make_async_copy(flat.at[slot + i], flat.at[slot + i], in_sem.at[slot + i]).wait()
        for v in range(wide):
            block = jnp.concatenate(
                [flat[slot + i, v, pl.ds(j, SUB, stride=tall), :] for i in range(2) for j in range(tall)]
                + [jnp.zeros((LANE - 2 * rows, LANE), jnp.float32)],
                axis=0,
            )
            turn[v * LANE : (v + 1) * LANE, :] = block.T
        for v in range(wide):
            block = turn[pl.ds(v, LANE, stride=wide), :].T
            for i in range(2):
                for j in range(tall):
                    start = (i * tall + j) * SUB
                    emit(i, j, v, block[start : start + SUB])

    def owner(b, j):
        half_tall = tall // 2
        return (tall * b + 2 * (j % half_tall) + (1 if j < half_tall else 0)) % levels

    def extra(b, t):
        u = lax.rem(t + levels * bins - tall * b, levels)
        return u < tall, u // 2 + (tall // 2) * (1 - lax.rem(u, 2))

    def place(b, v, j):
        tile = v * tall + j
        return (tile // main, tile % main) if v < wide - 1 else (owner(b, j), main)

    def index(b, v, j):
        t, i = place(b, v, j)
        return t * each + i

    def emit_tracer(b, j, v, tile):
        q[b, index(b, v, j)] = tile

    def emit_courant(i, j, v, tile):
        if i == 0:
            for n, c in enumerate(coefficients(tile)):
                cz[n, j, v + 1] = c
            return
        if j == tall - 1:
            tile = jnp.where(jnp.logical_and(last, band == bands - 1), 0.0, tile)
            ns[v : v + 1, :] = tile[SUB - 1 :, :]
        for n, c in enumerate(coefficients(tile)):
            cm[n, v, j + 1] = c

    def emit_fall(b, j, v, tile):
        t, i = place(b, v, j)
        fs[t * share + (b * main + i if i < main else bins * main + b % spare)] = tile

    with scope("spread"):
        spread(0, emit_tracer)
        spread(bins, emit_courant)
        for n in range(3):
            for j in range(tall):
                cz[n, j, 0] = pltpu.roll(cz[n, j, wide], 1, 1)

    north_row = pltpu.make_async_remote_copy(
        ns, nr, n_sem.at[0], n_sem.at[1], device_id={"lat": band + 1}, device_id_type=MESH
    )

    def halo(s, side, b):
        target = band + 1 if side == 0 else band - 1
        return pltpu.make_async_remote_copy(
            hs.at[side, s, b], hr.at[side, s, b], hs_sem.at[side], hr_sem.at[s % 2, side, b],
            device_id={"lat": target}, device_id_type=MESH,
        )

    def zonal(s, b, field):
        with scope("zonal"):
            for j in range(tall):
                own = [field[b, index(b, v, j)] for v in range(wide)]
                ext = jnp.stack(
                    [pltpu.roll(t, 1, 1) for t in own[-3:]] + own + [pltpu.roll(t, LANE - 1, 1) for t in own[:3]]
                )
                new = swept(ext, cz[0, j], cz[1, j], cz[2, j])
                for v in range(wide):
                    z[b, v * tall + j] = new[v]
                    if j < 3:
                        hs[1, s, b, pl.ds(j * wide + v, 1), :] = new[v][:1, :]
                    if j >= tall - 3:
                        hs[0, s, b, pl.ds((j - tall + 3) * wide + v, 1), :] = new[v][SUB - 1 :, :]

    def send_halo(s, b):
        @pl.when(has_north)
        def _():
            halo(s, 0, b).start()

        @pl.when(has_south)
        def _():
            halo(s, 1, b).start()

    def meridional(s, b, keep):
        with scope("halo"):
            @pl.when(has_south)
            def _():
                halo(s, 0, b).wait_recv()

            @pl.when(has_north)
            def _():
                halo(s, 1, b).wait_recv()

        with scope("meridional"):
            for v in range(wide):
                own = z[b, v * tall : (v + 1) * tall]
                below = [
                    jnp.where(first, hr[0, s, b, pl.ds(i * wide + v, 1), :], pltpu.roll(own[tall - 3 + i], 1, 0))
                    for i in range(3)
                ]
                above = [
                    jnp.where(last, hr[1, s, b, pl.ds(i * wide + v, 1), :], pltpu.roll(own[i], SUB - 1, 0))
                    for i in range(3)
                ]
                ext = jnp.concatenate([jnp.stack(below), own, jnp.stack(above)])
                new = swept(ext, cm[0, v], cm[1, v], cm[2, v])
                for j in range(tall):
                    keep(b, v, j, new[j])

    def keep_mass(b, v, j, tile):
        q[b, index(b, v, j)] = tile

    def keep_last(b, v, j, tile):
        q3[b, v * tall + j] = tile

    def copy_to(i, source, target, send, recv):
        return pltpu.make_async_remote_copy(
            source, target, send, recv, device_id={"lev": to(i)}, device_id_type=MESH
        )

    def either(condition, yes, no):
        @pl.when(condition)
        def _():
            yes()

        @pl.when(jnp.logical_not(condition))
        def _():
            no()

    def deal_fall(i):
        return copy_to(i, fs.at[pl.ds(to(i) * share, share)], rf.at[me], f_sem.at[0], f_sem.at[1])

    def deal_mass(b, i):
        t = to(i)
        send, recv = w_sem.at[0, b], w_sem.at[1, b]
        either(
            extra(b, t)[0],
            copy_to(i, q.at[b, pl.ds(t * each, each)], rw.at[b, me], send, recv).start,
            copy_to(i, q.at[b, pl.ds(t * each, main)], rw.at[b, me, pl.ds(0, main)], send, recv).start,
        )

    def give_back(b, i):
        t = to(i)
        send, recv = b_sem.at[0, b], b_sem.at[1, b]
        either(
            extra(b, me)[0],
            copy_to(i, so.at[b, t], q2.at[b, pl.ds(me * each, each)], send, recv).start,
            copy_to(i, so.at[b, t, pl.ds(0, main)], q2.at[b, pl.ds(me * each, main)], send, recv).start,
        )

    def settler(b, sems, side):
        full, part = rw.at[b, pl.ds(0, n_moves)], rw.at[b, pl.ds(0, n_moves), pl.ds(0, main)]
        name = "wait_recv" if side else "wait_send"
        either(
            extra(b, me)[0],
            getattr(copy_to(0, full, full, sems.at[0, b], sems.at[1, b]), name),
            getattr(copy_to(0, part, part, sems.at[0, b], sems.at[1, b]), name),
        )

    def holder(b, sems, side):
        count = n_moves * main + tall
        few, many = q.at[b, pl.ds(0, count - 1)], q.at[b, pl.ds(0, count)]
        name = "wait_recv" if side else "wait_send"
        either(
            extra(b, me)[0],
            getattr(copy_to(0, few, few, sems.at[0, b], sems.at[1, b]), name),
            getattr(copy_to(0, many, many, sems.at[0, b], sems.at[1, b]), name),
        )

    all_fall = copy_to(0, rf.at[pl.ds(0, n_moves)], rf.at[pl.ds(0, n_moves)], f_sem.at[0], f_sem.at[1])

    def send_fall(some):
        for i in some:
            deal_fall(i).start()

    per_step = -(-len(other_half) // HSUB)

    for b in range(bins):
        zonal(0, b, q)
    with scope("barrier"):
        pl.semaphore_wait(barrier, n_moves + has_south.astype(jnp.int32) + has_north.astype(jnp.int32))

    @pl.when(has_north)
    def _():
        north_row.start()

    for b in range(bins):
        send_halo(0, b)
    with scope("spread_fall"):
        spread(bins + 2, emit_fall)
    with scope("send_fall"):
        send_fall(same_half + other_half[:per_step])
    for i in range(share):
        rf[me, i] = fs[me * share + i]

    with scope("north_row"):
        @pl.when(has_south)
        def _():
            north_row.wait_recv()

        for v in range(wide):
            below = coefficients(nr[v : v + 1, :])
            for n in range(3):
                cm[n, v, 0] = jnp.where(first, below[n], pltpu.roll(cm[n, v, tall], 1, 0))
    for b in range(bins):
        meridional(0, b, keep_mass)

    for s in range(1, HSUB):
        for b in range(bins):
            zonal(s, b, q)
            send_halo(s, b)
        send_fall(other_half[s * per_step : (s + 1) * per_step])
        for b in range(bins):
            meridional(s, b, keep_mass)
            if s == HSUB - 1:
                for i in range(n_moves):
                    deal_mass(b, i)

    for b in range(bins):
        owned, extra_j = extra(b, me)
        for i in range(main):
            rw[b, me, i] = q[b, me * each + i]

        @pl.when(owned)
        def _():
            rw[b, me, main] = q[b, me * each + main]

        if b == 0:
            with scope("wait_fall"):
                all_fall.wait_recv()
        with scope("wait_mass"):
            settler(b, w_sem, 1)

        def settle(i, j):
            mass = rw[b, :, i]
            half = 0.5 * rf[:, b * main + i if i < main else bins * main + b % spare]
            fallen = jnp.zeros((SUB, LANE), jnp.float32)
            for _ in range(SETTLE_SUBSTEPS):
                flux = (mass * half) * (2.0 + jnp.tanh(mass))
                inflow = jnp.concatenate([jnp.zeros((1, SUB, LANE), jnp.float32), flux[:-1]], axis=0)
                mass = (mass + inflow) - flux
                fallen = fallen + flux[levels - 1]
            so[b, :, i] = mass
            dblk[pl.ds((b * tall + j) * SUB, SUB), :] = fallen

        with scope("settle"):
            for i in range(main):
                settle(i, lax.rem(me * main + i, tall))

            @pl.when(owned)
            def _():
                settle(main, extra_j)

        with scope("give_back"):
            for i in range(n_moves):
                give_back(b, i)
        for i in range(main):
            q2[b, me * each + i] = so[b, me, i]

        @pl.when(owned)
        def _():
            q2[b, me * each + main] = so[b, me, main]

    dts[...] = dblk[...].T

    def drop(i):
        return pltpu.make_async_remote_copy(
            dts.at[pl.ds(to(i) * lanes_each, lanes_each)], dr.at[me], d_sem.at[0], d_sem.at[1],
            device_id={"lev": to(i)}, device_id_type=MESH,
        )

    for i in range(n_moves):
        drop(i).start()
    dr[me] = dts[pl.ds(me * lanes_each, lanes_each), :]

    for b in range(bins):
        with scope("wait_back"):
            holder(b, b_sem, 1)
        zonal(HSUB, b, q2)
        send_halo(HSUB, b)

    with scope("deposit"):
        all_drops = copy_to(0, dr.at[pl.ds(0, n_moves)], dr.at[pl.ds(0, n_moves)], d_sem.at[0], d_sem.at[1])
        all_drops.wait_recv()
        column = lax.broadcasted_iota(jnp.int32, (lanes_each, LANE), 1) // SUB
        low_rows = lax.rem(column, tall) < tall // 2
        for v in range(wide - 1):
            turn[pl.ds(v, lanes_each, stride=wide), :] = jnp.where(low_rows, dr[2 * v], dr[2 * v + 1])
        tail = jnp.zeros((lanes_each, LANE), jnp.float32)
        for g, (b, j) in enumerate(groups):
            t = (tall * b + 2 * (j % (tall // 2)) + (1 if j < tall // 2 else 0)) % levels
            tail = jnp.where(column == g, dr[t], tail)
        turn[pl.ds(wide - 1, lanes_each, stride=wide), :] = tail
        block = turn[:LANE, :].T
        for g, (b, j) in enumerate(groups):
            flat[bins + b, 0, pl.ds(j, SUB, stride=tall), :] = block[g * SUB : (g + 1) * SUB]
        for b in range(bins):
            deposit[b] = flat[bins + b, 0][:, :chunk]

    for b in range(bins):
        meridional(HSUB, b, keep_last)

    written = [
        pltpu.make_async_copy(flat.at[b, v], out.at[b, :, pl.ds(v * LANE, LANE)], out_sem.at[0])
        for v in range(wide)
        for b in range(bins)
    ]
    with scope("gather"):
        for v in range(wide):
            block = jnp.concatenate(
                [q3[b, v * tall + j] for b, j in groups] + [jnp.zeros((LANE - bins * rows, LANE), jnp.float32)], axis=0
            )
            turn[pl.ds(v, LANE, stride=wide), :] = block.T
        for v in range(wide):
            block = turn[v * LANE : (v + 1) * LANE, :].T
            for g, (b, j) in enumerate(groups):
                flat[b, v, pl.ds(j, SUB, stride=tall), :] = block[g * SUB : (g + 1) * SUB]
            for copy in written[v * bins : (v + 1) * bins]:
                copy.start()

    with scope("sent"):
        @pl.when(has_north)
        def _():
            north_row.wait_send()

        for side, there in ((0, has_north), (1, has_south)):
            @pl.when(there)
            def _():
                pltpu.make_async_remote_copy(
                    hs.at[side], hr.at[side], hs_sem.at[side], hr_sem.at[0, side, 0],
                    device_id={"lat": band + 1 if side == 0 else band - 1}, device_id_type=MESH,
                ).wait_send()

        all_fall.wait_send()
        for b in range(bins):
            holder(b, w_sem, 0)
            settler(b, b_sem, 0)
        all_drops.wait_send()
    with scope("written"):
        pltpu.make_async_copy(flat.at[pl.ds(0, bins)], flat.at[pl.ds(0, bins)], out_sem.at[0]).wait()


def on_device(bands, levels, tracer, east, north, fall):
    bins, _, rows, width = tracer.shape
    tall, wide = rows // SUB, width // LANE
    chunk = width // levels
    main = tall * (wide - 1) // levels
    each = main + 1
    share = main * bins + (1 if bins * tall <= levels else bins)
    edge = -(-3 * wide // SUB) * SUB
    line = -(-wide // SUB) * SUB
    steps = HSUB + 1
    f32 = jnp.float32
    field = VMEM((bins, wide * tall, SUB, LANE), f32)
    dealt = VMEM((bins, levels * each, SUB, LANE), f32)
    columns = VMEM((bins, levels, each, SUB, LANE), f32)
    out, deposit = pl.pallas_call(
        functools.partial(kernel, bands, levels),
        out_shape=(
            jax.ShapeDtypeStruct((bins, rows, width), f32),
            jax.ShapeDtypeStruct((bins, rows, chunk), f32),
        ),
        in_specs=[pl.BlockSpec(memory_space=pltpu.HBM)] * 4,
        out_specs=(pl.BlockSpec(memory_space=pltpu.HBM), pl.BlockSpec(memory_space=VMEM)),
        scratch_shapes=[
            VMEM((2 + 2 * bins, wide, rows, LANE), f32),
            VMEM((width, LANE), f32),
            dealt,
            field,
            dealt,
            field,
            VMEM((levels * share, SUB, LANE), f32),
            VMEM((3, tall, wide + 1, SUB, LANE), f32),
            VMEM((3, wide, tall + 1, SUB, LANE), f32),
            VMEM((2, steps, bins, edge, LANE), f32),
            VMEM((2, steps, bins, edge, LANE), f32),
            VMEM((line, LANE), f32),
            VMEM((line, LANE), f32),
            VMEM((levels, share, SUB, LANE), f32),
            columns,
            columns,
            VMEM((LANE, LANE), f32),
            VMEM((LANE, LANE), f32),
            VMEM((levels, LANE // levels, LANE), f32),
            DMA((2 + 2 * bins,)),
            DMA((1,)),
            DMA((2,)),
            DMA((2, 2, bins)),
            DMA((2,)),
            DMA((2,)),
            DMA((2, bins)),
            DMA((2, bins)),
            DMA((2,)),
        ],
        compiler_params=pltpu.CompilerParams(collective_id=0, has_side_effects=True),
        cost_estimate=pl.CostEstimate(flops=50000000, bytes_accessed=3000000, transcendentals=700000),
    )(
        tracer.reshape(bins, rows, width),
        east.reshape(rows, width),
        north.reshape(rows, width),
        fall.reshape(bins, rows, width),
    )
    return out.reshape(tracer.shape), deposit


def solution(mesh):
    in_specs = (
        P(None, "lev", "lat", None),
        P("lev", "lat", None),
        P("lev", "lat", None),
        P(None, "lev", "lat", None),
    )
    out_specs = (P(None, "lev", "lat", None), P(None, "lat", "lev"))
    return jax.shard_map(
        functools.partial(on_device, mesh.shape["lat"], mesh.shape["lev"]),
        mesh=mesh, in_specs=in_specs, out_specs=out_specs, check_vma=False,
    )
```

time: 145 us -> 48 us (0.33)
  other arithmetic: 49.1 us -> 0 us
  Pallas kernels: 0 us -> 44.4 us
  starting transfers between devices: 36.6 us -> 0 us
  local copies, waits for them, and re-layouts: 37.9 us -> 2.44 us
  waiting for transfers between devices: 18.6 us -> 0 us
    pallas_call x0 -> x1, Pallas kernels: none -> 44.4 us  [on_device(): pl.pallas_call(functools.partial(kernel, bands, levels), out_shape=(jax.S...]
    ppermute x5 -> x0, starting transfers between devices: 19.5 us -> none  [the longest x2 7.44 us: extended_2(): lax.ppermute(lax.slice_in_dim(block, block.shape[dim] - width, None, axis...]
    unnamed x113 -> x4, local copies, waits for them, and re-layouts: 21.7 us -> 2.44 us
    mul x30 -> x0, other arithmetic: 17.9 us -> none  [the longest x18 9.92 us: sweep(): face_flux_values = courant * jnp.where(courant >= 0, from_west, from_east)]
    all_to_all x3 -> x0, starting transfers between devices: 17.1 us -> none  [the longest x1 6.57 us: on_device(): lax.all_to_all(field, 'lev', split_axis=3, concat_axis=1, tiled=True)]
    all_to_all x3 -> x0, waiting for transfers between devices: 16 us -> none  [the longest x1 12.9 us: columns_settle(): lax.all_to_all(settled.reshape(shape_full), 'lev', split_axis=1, concat_a...]
    ge x10 -> x0, other arithmetic: 6.78 us -> none  [sweep(): face_flux_values = courant * jnp.where(courant >= 0, from_west, from_east)]
    slice x17 -> x0, local copies, waits for them, and re-layouts: 6.58 us -> none  [the longest x14 5.07 us: window_for_cell(): return lax.slice_in_dim(source, start, start + length, axis=axis_dim)]
  transfers between devices with their start and end apart: 8 -> 0, of which waited for: 3 -> 0; matrix products, arithmetic and copies ran while one was open for 42% -> 0% of each run, Pallas kernels for 0% -> 0%
where the time goes in v2:
time: 48 us; the launch traced here: 47.5 us
  Pallas kernels  44.4 us (92%)
  local copies, waits for them, and re-layouts  2.44 us (5%)
  between operations  0.65 us (1%)
    pallas_call x1, Pallas kernels, on_device(): pl.pallas_call(functools.partial(kernel, bands, levels), out_shape=(jax.S...  44.4 us
    unnamed x4, local copies, waits for them, and re-layouts  2.44 us

profile of v2, /device:TPU:104, one launch (start us, length us, event | category | flops | bytes accessed | tf_op | source)
XLA Modules:
  0.0 47.5 jit_solution(8914954234112073462)
XLA Ops:
  0.6 44.4 %shard_map.59 = (f32[2,48,1152]{2,1,0:T(8,128)}, f32[2,48,72]{2,1,0:T(8,128)}) custom-call(f32[2,48,1152]{2,1,0:T(8,128)} %bitcast.8, f32[48,1152]{1,0:T(8,128)} %bitcast.10, f32[48,1152]{1,0:T(8,128)} %bitcast.11, f32[2,48,1152]{2,1,0:T(8,128)} %bitcast.9), custom_call_target="tpu_custom_call" | custom-call | flops 50000000 | bytes 3000000 | tf_op jit(solution)/shard_map/pallas_call | solution.py:493
  45.1 0.0 copy-start
  45.1 1.8 %copy.9 = f32[2,1,48,1152]{3,2,1,0:T(8,128)} copy(f32[2,1,48,1152]{3,2,1,0:T(8,128)} %bitcast.7) | data formatting | bytes 884736
  46.9 0.0 copy-done
  46.9 0.6 %copy.10 = f32[2,48,72]{2,1,0:T(8,128)} copy(f32[2,48,72]{2,1,0:T(8,128)S(1)} %copy-done) | data formatting | bytes 55296
Async XLA Ops:
  45.1 1.8 %copy-start = (f32[2,48,72]{2,1,0:T(8,128)S(1)}, f32[2,48,72]{2,1,0:T(8,128)}, u32[]{:S(2)}) copy-start(f32[2,48,72]{2,1,0:T(8,128)} %get-tuple-element.11) | copy-start | bytes 82948

commit v3 on v2

--- a/solution.py
+++ b/solution.py
@@ -41,8 +41,8 @@
 def kernel(
     bands, levels,
     tracer, east, north, fall, out, deposit,
-    flat, turn, q, z, q2, q3, fs, cz, cm, hs, hr, ns, nr, rf, rw, so, dblk, dts, dr,
-    in_sem, out_sem, hs_sem, hr_sem, n_sem, f_sem, w_sem, b_sem, d_sem,
+    flat, turn, q, z, q2, q3, fs, cz, czp, cm, p, zp, hs, hr, hsf, hrf, cs, cr, pe, rf, rw, so, dblk, dts, dr,
+    in_sem, out_sem, hs_sem, hr_sem, c_sem, f_sem, w_sem, b_sem, d_sem,
 ):
     bins, rows, width = tracer.shape
     tall = rows // SUB
@@ -109,18 +109,14 @@
         for copy in copies:
             copy.start()
 
-    @pl.when(band == 0)
-    def _():
-        nr[...] = jnp.zeros_like(nr)
-        for s in range(HSUB + 1):
+    for side, beyond in ((0, band == 0), (1, band == bands - 1)):
+        @pl.when(beyond)
+        def _():
+            cr[side] = jnp.zeros(cr.shape[1:], jnp.float32)
             for b in range(bins):
-                hr[0, s, b] = jnp.zeros(hr.shape[3:], jnp.float32)
-
-    @pl.when(band == bands - 1)
-    def _():
-        for s in range(HSUB + 1):
-            for b in range(bins):
-                hr[1, s, b] = jnp.zeros(hr.shape[3:], jnp.float32)
+                hrf[side, b] = jnp.zeros(hrf.shape[2:], jnp.float32)
+                for e in range(2):
+                    hr[side, e, b] = jnp.zeros(hr.shape[3:], jnp.float32)
 
     dblk[...] = jnp.zeros_like(dblk)
 
@@ -161,15 +157,18 @@
         q[b, index(b, v, j)] = tile
 
     def emit_courant(i, j, v, tile):
-        if i == 0:
-            for n, c in enumerate(coefficients(tile)):
+        if i == 1 and j == tall - 1:
+            tile = jnp.where(jnp.logical_and(last, band == bands - 1), 0.0, tile)
+        sent, at_row = (3, 4) if i == 0 else (4, 0)
+        if j >= tall - sent:
+            cs[0, pl.ds((at_row + j - tall + sent) * wide + v, 1), :] = tile[SUB - 1 :, :]
+        if j < 3:
+            cs[1, pl.ds((at_row + j) * wide + v, 1), :] = tile[:1, :]
+        for n, c in enumerate(coefficients(tile)):
+            if i == 0:
                 cz[n, j, v + 1] = c
-            return
-        if j == tall - 1:
-            tile = jnp.where(jnp.logical_and(last, band == bands - 1), 0.0, tile)
-            ns[v : v + 1, :] = tile[SUB - 1 :, :]
-        for n, c in enumerate(coefficients(tile)):
-            cm[n, v, j + 1] = c
+            else:
+                cm[n, v, j + 4] = c
 
     def emit_fall(b, j, v, tile):
         t, i = place(b, v, j)
@@ -182,66 +181,97 @@
             for j in range(tall):
                 cz[n, j, 0] = pltpu.roll(cz[n, j, wide], 1, 1)
 
-    north_row = pltpu.make_async_remote_copy(
-        ns, nr, n_sem.at[0], n_sem.at[1], device_id={"lat": band + 1}, device_id_type=MESH
-    )
-
-    def halo(s, side, b):
-        target = band + 1 if side == 0 else band - 1
+    def near(side):
+        return {"lat": band + 1 if side == 0 else band - 1}
+
+    def courants(side):
         return pltpu.make_async_remote_copy(
-            hs.at[side, s, b], hr.at[side, s, b], hs_sem.at[side], hr_sem.at[s % 2, side, b],
-            device_id={"lat": target}, device_id_type=MESH,
-        )
-
-    def zonal(s, b, field):
+            cs.at[side], cr.at[side], c_sem.at[0, side], c_sem.at[1, side], device_id=near(side), device_id_type=MESH
+        )
+
+    def halo(e, side, b):
+        source, target = (hs.at[side, e, b], hr.at[side, e, b]) if e < 2 else (hsf.at[side, b], hrf.at[side, b])
+        return pltpu.make_async_remote_copy(
+            source, target, hs_sem.at[e // 2, side], hr_sem.at[e, side, b], device_id=near(side), device_id_type=MESH
+        )
+
+    def zonal_row(own, c0, c1, c2):
+        ext = [pltpu.roll(t, 1, 1) for t in own[-3:]] + own + [pltpu.roll(t, LANE - 1, 1) for t in own[:3]]
+        return swept(jnp.stack(ext), c0, c1, c2)
+
+    def zonal(e, b, field):
         with scope("zonal"):
             for j in range(tall):
-                own = [field[b, index(b, v, j)] for v in range(wide)]
-                ext = jnp.stack(
-                    [pltpu.roll(t, 1, 1) for t in own[-3:]] + own + [pltpu.roll(t, LANE - 1, 1) for t in own[:3]]
-                )
-                new = swept(ext, cz[0, j], cz[1, j], cz[2, j])
+                new = zonal_row([field[b, index(b, v, j)] for v in range(wide)], cz[0, j], cz[1, j], cz[2, j])
                 for v in range(wide):
                     z[b, v * tall + j] = new[v]
-                    if j < 3:
-                        hs[1, s, b, pl.ds(j * wide + v, 1), :] = new[v][:1, :]
-                    if j >= tall - 3:
-                        hs[0, s, b, pl.ds((j - tall + 3) * wide + v, 1), :] = new[v][SUB - 1 :, :]
-
-    def send_halo(s, b):
+                    low, high = new[v][:1, :], new[v][SUB - 1 :, :]
+                    if e in (0, 1):
+                        hs[1, e, b, pl.ds(j * wide + v, 1), :] = low
+                        hs[0, e, b, pl.ds(j * wide + v, 1), :] = high
+                    elif e == 2 and j < 3:
+                        hsf[1, b, pl.ds(j * wide + v, 1), :] = low
+                    elif e == 2 and j >= tall - 3:
+                        hsf[0, b, pl.ds((j - tall + 3) * wide + v, 1), :] = high
+            if e is None:
+                new = zonal_row([p[b, v] for v in range(wide)], czp[0], czp[1], czp[2])
+                for v in range(wide):
+                    zp[b, v] = new[v]
+
+    def send_halo(e, b):
         @pl.when(has_north)
         def _():
-            halo(s, 0, b).start()
+            halo(e, 0, b).start()
 
         @pl.when(has_south)
         def _():
-            halo(s, 1, b).start()
-
-    def meridional(s, b, keep):
+            halo(e, 1, b).start()
+
+    def wait_halo(e, b):
         with scope("halo"):
             @pl.when(has_south)
             def _():
-                halo(s, 0, b).wait_recv()
+                halo(e, 0, b).wait_recv()
 
             @pl.when(has_north)
             def _():
-                halo(s, 1, b).wait_recv()
-
+                halo(e, 1, b).wait_recv()
+
+    def extended(own, lows, highs):
+        n = len(lows)
+        below = [jnp.where(first, lows[i], pltpu.roll(own[tall - n + i], 1, 0)) for i in range(n)]
+        above = [jnp.where(last, highs[i], pltpu.roll(own[i], SUB - 1, 0)) for i in range(n)]
+        return jnp.stack(below + own + above)
+
+    def meridional_wide(e, b):
+        wait_halo(e, b)
+        with scope("meridional_wide"):
+            for v in range(wide):
+                own = [z[b, v * tall + j] for j in range(tall)]
+                lows = [hr[0, e, b, pl.ds(i * wide + v, 1), :] for i in range(tall)]
+                highs = [hr[1, e, b, pl.ds(i * wide + v, 1), :] for i in range(tall)]
+                new = swept(extended(own, lows, highs), cm[0, v], cm[1, v], cm[2, v])
+                for j in range(tall):
+                    q[b, index(b, v, j)] = new[j + 3]
+                for i in range(3):
+                    p[b, v, i : i + 1, :] = new[i][:1, :]
+                    p[b, v, i + 3 : i + 4, :] = new[tall + 3 + i][SUB - 1 :, :]
+
+    def meridional(b, rows_of, keep):
         with scope("meridional"):
             for v in range(wide):
-                own = z[b, v * tall : (v + 1) * tall]
-                below = [
-                    jnp.where(first, hr[0, s, b, pl.ds(i * wide + v, 1), :], pltpu.roll(own[tall - 3 + i], 1, 0))
-                    for i in range(3)
-                ]
-                above = [
-                    jnp.where(last, hr[1, s, b, pl.ds(i * wide + v, 1), :], pltpu.roll(own[i], SUB - 1, 0))
-                    for i in range(3)
-                ]
-                ext = jnp.concatenate([jnp.stack(below), own, jnp.stack(above)])
-                new = swept(ext, cm[0, v], cm[1, v], cm[2, v])
+                own = [z[b, v * tall + j] for j in range(tall)]
+                lows, highs = rows_of(b, v)
+                c0, c1, c2 = [cm[n, v, 3 : tall + 4] for n in range(3)]
+                new = swept(extended(own, lows, highs), c0, c1, c2)
                 for j in range(tall):
                     keep(b, v, j, new[j])
+
+    def rows_kept(b, v):
+        return [zp[b, v, i : i + 1, :] for i in range(3)], [zp[b, v, i + 3 : i + 4, :] for i in range(3)]
+
+    def rows_sent(b, v):
+        return [[hrf[side, b, pl.ds(i * wide + v, 1), :] for i in range(3)] for side in range(2)]
 
     def keep_mass(b, v, j, tile):
         q[b, index(b, v, j)] = tile
@@ -309,46 +339,68 @@
         for i in some:
             deal_fall(i).start()
 
-    per_step = -(-len(other_half) // HSUB)
-
+    for b in range(bins):
+        p[b] = jnp.zeros(p.shape[1:], jnp.float32)
+    pe[...] = jnp.zeros_like(pe)
     for b in range(bins):
         zonal(0, b, q)
+    with scope("spread_fall"):
+        spread(bins + 2, emit_fall)
     with scope("barrier"):
         pl.semaphore_wait(barrier, n_moves + has_south.astype(jnp.int32) + has_north.astype(jnp.int32))
 
     @pl.when(has_north)
     def _():
-        north_row.start()
+        courants(0).start()
+
+    @pl.when(has_south)
+    def _():
+        courants(1).start()
 
     for b in range(bins):
         send_halo(0, b)
-    with scope("spread_fall"):
-        spread(bins + 2, emit_fall)
     with scope("send_fall"):
-        send_fall(same_half + other_half[:per_step])
+        send_fall(same_half + other_half)
     for i in range(share):
         rf[me, i] = fs[me * share + i]
 
-    with scope("north_row"):
+    with scope("courants"):
         @pl.when(has_south)
         def _():
-            north_row.wait_recv()
-
+            courants(0).wait_recv()
+
+        @pl.when(has_north)
+        def _():
+            courants(1).wait_recv()
+
+    with scope("edge_coefficients"):
         for v in range(wide):
-            below = coefficients(nr[v : v + 1, :])
-            for n in range(3):
-                cm[n, v, 0] = jnp.where(first, below[n], pltpu.roll(cm[n, v, tall], 1, 0))
-    for b in range(bins):
-        meridional(0, b, keep_mass)
-
-    for s in range(1, HSUB):
+            for i in range(4):
+                low = coefficients(cr[0, pl.ds(i * wide + v, 1), :])
+                for n in range(3):
+                    cm[n, v, i] = jnp.where(first, low[n], pltpu.roll(cm[n, v, i + tall], 1, 0))
+            for i in range(3):
+                high = coefficients(cr[1, pl.ds(i * wide + v, 1), :])
+                for n in range(3):
+                    cm[n, v, tall + 4 + i] = jnp.where(last, high[n], pltpu.roll(cm[n, v, i + 4], SUB - 1, 0))
+                pe[v, i : i + 1, :] = cr[0, pl.ds((4 + i) * wide + v, 1), :]
+                pe[v, i + 3 : i + 4, :] = cr[1, pl.ds((4 + i) * wide + v, 1), :]
+        for v in range(wide):
+            for n, c in enumerate(coefficients(pe[v])):
+                czp[n, v + 1] = c
+        for n in range(3):
+            czp[n, 0] = pltpu.roll(czp[n, wide], 1, 1)
+
+    for e in range(HSUB // 2):
+        if e:
+            for b in range(bins):
+                zonal(e, b, q)
+                send_halo(e, b)
         for b in range(bins):
-            zonal(s, b, q)
-            send_halo(s, b)
-        send_fall(other_half[s * per_step : (s + 1) * per_step])
-        for b in range(bins):
-            meridional(s, b, keep_mass)
-            if s == HSUB - 1:
+            meridional_wide(e, b)
+            zonal(None, b, q)
+            meridional(b, rows_kept, keep_mass)
+            if e == HSUB // 2 - 1:
                 for i in range(n_moves):
                     deal_mass(b, i)
 
@@ -412,8 +464,8 @@
     for b in range(bins):
         with scope("wait_back"):
             holder(b, b_sem, 1)
-        zonal(HSUB, b, q2)
-        send_halo(HSUB, b)
+        zonal(2, b, q2)
+        send_halo(2, b)
 
     with scope("deposit"):
         all_drops = copy_to(0, dr.at[pl.ds(0, n_moves)], dr.at[pl.ds(0, n_moves)], d_sem.at[0], d_sem.at[1])
@@ -434,7 +486,8 @@
             deposit[b] = flat[bins + b, 0][:, :chunk]
 
     for b in range(bins):
-        meridional(HSUB, b, keep_last)
+        wait_halo(2, b)
+        meridional(b, rows_sent, keep_last)
 
     written = [
         pltpu.make_async_copy(flat.at[b, v], out.at[b, :, pl.ds(v * LANE, LANE)], out_sem.at[0])
@@ -455,17 +508,15 @@
                 copy.start()
 
     with scope("sent"):
-        @pl.when(has_north)
-        def _():
-            north_row.wait_send()
-
         for side, there in ((0, has_north), (1, has_south)):
             @pl.when(there)
             def _():
-                pltpu.make_async_remote_copy(
-                    hs.at[side], hr.at[side], hs_sem.at[side], hr_sem.at[0, side, 0],
-                    device_id={"lat": band + 1 if side == 0 else band - 1}, device_id_type=MESH,
-                ).wait_send()
+                courants(side).wait_send()
+                for kind, (source, target) in enumerate(((hs, hr), (hsf, hrf))):
+                    pltpu.make_async_remote_copy(
+                        source.at[side], target.at[side], hs_sem.at[kind, side], hr_sem.at[0, side, 0],
+                        device_id=near(side), device_id_type=MESH,
+                    ).wait_send()
 
         all_fall.wait_send()
         for b in range(bins):
@@ -483,9 +534,9 @@
     main = tall * (wide - 1) // levels
     each = main + 1
     share = main * bins + (1 if bins * tall <= levels else bins)
-    edge = -(-3 * wide // SUB) * SUB
-    line = -(-wide // SUB) * SUB
-    steps = HSUB + 1
+    def lines(n):
+        return -(-n * wide // SUB) * SUB
+
     f32 = jnp.float32
     field = VMEM((bins, wide * tall, SUB, LANE), f32)
     dealt = VMEM((bins, levels * each, SUB, LANE), f32)
@@ -507,11 +558,17 @@
             field,
             VMEM((levels * share, SUB, LANE), f32),
             VMEM((3, tall, wide + 1, SUB, LANE), f32),
-            VMEM((3, wide, tall + 1, SUB, LANE), f32),
-            VMEM((2, steps, bins, edge, LANE), f32),
-            VMEM((2, steps, bins, edge, LANE), f32),
-            VMEM((line, LANE), f32),
-            VMEM((line, LANE), f32),
+            VMEM((3, wide + 1, SUB, LANE), f32),
+            VMEM((3, wide, tall + 7, SUB, LANE), f32),
+            VMEM((bins, wide, SUB, LANE), f32),
+            VMEM((bins, wide, SUB, LANE), f32),
+            VMEM((2, 2, bins, lines(tall), LANE), f32),
+            VMEM((2, 2, bins, lines(tall), LANE), f32),
+            VMEM((2, bins, lines(3), LANE), f32),
+            VMEM((2, bins, lines(3), LANE), f32),
+            VMEM((2, lines(7), LANE), f32),
+            VMEM((2, lines(7), LANE), f32),
+            VMEM((wide, SUB, LANE), f32),
             VMEM((levels, share, SUB, LANE), f32),
             columns,
             columns,
@@ -520,9 +577,9 @@
             VMEM((levels, LANE // levels, LANE), f32),
             DMA((2 + 2 * bins,)),
             DMA((1,)),
-            DMA((2,)),
-            DMA((2, 2, bins)),
-            DMA((2,)),
+            DMA((2, 2)),
+            DMA((3, 2, bins)),
+            DMA((2, 2)),
             DMA((2,)),
             DMA((2, bins)),
             DMA((2, bins)),

time: 48 us -> 45.6 us (0.950)
  the two profiles are of different devices: /device:TPU:104 before, /device:TPU:112 now
where the time goes in v3:
time: 45.6 us; the launch traced here: 45.4 us
  Pallas kernels  42.3 us (93%)
  local copies, waits for them, and re-layouts  2.44 us (5%)
  between operations  0.65 us (1%)
    pallas_call x1, Pallas kernels, on_device(): pl.pallas_call(functools.partial(kernel, bands, levels), out_shape=(jax.S...  42.3 us
    unnamed x4, local copies, waits for them, and re-layouts  2.44 us

profile of v3, /device:TPU:112, one launch (start us, length us, event | category | flops | bytes accessed | tf_op | source)
XLA Modules:
  0.0 45.4 jit_solution(9107344278630275532)
XLA Ops:
  0.6 42.3 %shard_map.59 = (f32[2,48,1152]{2,1,0:T(8,128)}, f32[2,48,72]{2,1,0:T(8,128)}) custom-call(f32[2,48,1152]{2,1,0:T(8,128)} %bitcast.8, f32[48,1152]{1,0:T(8,128)} %bitcast.10, f32[48,1152]{1,0:T(8,128)} %bitcast.11, f32[2,48,1152]{2,1,0:T(8,128)} %bitcast.9), custom_call_target="tpu_custom_call" | custom-call | flops 50000000 | bytes 3000000 | tf_op jit(solution)/shard_map/pallas_call | solution.py:544
  42.9 0.0 copy-start
  43.0 1.8 %copy.9 = f32[2,1,48,1152]{3,2,1,0:T(8,128)} copy(f32[2,1,48,1152]{3,2,1,0:T(8,128)} %bitcast.7) | data formatting | bytes 884736
  44.8 0.0 copy-done
  44.8 0.6 %copy.10 = f32[2,48,72]{2,1,0:T(8,128)} copy(f32[2,48,72]{2,1,0:T(8,128)S(1)} %copy-done) | data formatting | bytes 55296
Async XLA Ops:
  42.9 1.8 %copy-start = (f32[2,48,72]{2,1,0:T(8,128)S(1)}, f32[2,48,72]{2,1,0:T(8,128)}, u32[]{:S(2)}) copy-start(f32[2,48,72]{2,1,0:T(8,128)} %get-tuple-element.11) | copy-start | bytes 82948

commit v4 on v3

--- a/solution.py
+++ b/solution.py
@@ -42,7 +42,7 @@
     bands, levels,
     tracer, east, north, fall, out, deposit,
     flat, turn, q, z, q2, q3, fs, cz, czp, cm, p, zp, hs, hr, hsf, hrf, cs, cr, pe, rf, rw, so, dblk, dts, dr,
-    in_sem, out_sem, hs_sem, hr_sem, c_sem, f_sem, w_sem, b_sem, d_sem,
+    in_sem, hs_sem, hr_sem, c_sem, f_sem, w_sem, b_sem, d_sem,
 ):
     bins, rows, width = tracer.shape
     tall = rows // SUB
@@ -245,6 +245,8 @@
 
     def meridional_wide(e, b):
         wait_halo(e, b)
+        if e == 0 and b == bins - 1:
+            send_fall(other_half[:3])
         with scope("meridional_wide"):
             for v in range(wide):
                 own = [z[b, v * tall + j] for j in range(tall)]
@@ -359,8 +361,6 @@
 
     for b in range(bins):
         send_halo(0, b)
-    with scope("send_fall"):
-        send_fall(same_half + other_half)
     for i in range(share):
         rf[me, i] = fs[me * share + i]
 
@@ -396,6 +396,7 @@
             for b in range(bins):
                 zonal(e, b, q)
                 send_halo(e, b)
+            send_fall(other_half[3:] + same_half)
         for b in range(bins):
             meridional_wide(e, b)
             zonal(None, b, q)
@@ -466,6 +467,10 @@
             holder(b, b_sem, 1)
         zonal(2, b, q2)
         send_halo(2, b)
+
+    for b in range(bins):
+        wait_halo(2, b)
+        meridional(b, rows_sent, keep_last)
 
     with scope("deposit"):
         all_drops = copy_to(0, dr.at[pl.ds(0, n_moves)], dr.at[pl.ds(0, n_moves)], d_sem.at[0], d_sem.at[1])
@@ -485,15 +490,6 @@
         for b in range(bins):
             deposit[b] = flat[bins + b, 0][:, :chunk]
 
-    for b in range(bins):
-        wait_halo(2, b)
-        meridional(b, rows_sent, keep_last)
-
-    written = [
-        pltpu.make_async_copy(flat.at[b, v], out.at[b, :, pl.ds(v * LANE, LANE)], out_sem.at[0])
-        for v in range(wide)
-        for b in range(bins)
-    ]
     with scope("gather"):
         for v in range(wide):
             block = jnp.concatenate(
@@ -504,8 +500,8 @@
             block = turn[v * LANE : (v + 1) * LANE, :].T
             for g, (b, j) in enumerate(groups):
                 flat[b, v, pl.ds(j, SUB, stride=tall), :] = block[g * SUB : (g + 1) * SUB]
-            for copy in written[v * bins : (v + 1) * bins]:
-                copy.start()
+            for b in range(bins):
+                out[b, :, v * LANE : (v + 1) * LANE] = flat[b, v]
 
     with scope("sent"):
         for side, there in ((0, has_north), (1, has_south)):
@@ -523,9 +519,6 @@
             holder(b, w_sem, 0)
             settler(b, b_sem, 0)
         all_drops.wait_send()
-    with scope("written"):
-        pltpu.make_async_copy(flat.at[pl.ds(0, bins)], flat.at[pl.ds(0, bins)], out_sem.at[0]).wait()
-
 
 def on_device(bands, levels, tracer, east, north, fall):
     bins, _, rows, width = tracer.shape
@@ -548,7 +541,7 @@
             jax.ShapeDtypeStruct((bins, rows, chunk), f32),
         ),
         in_specs=[pl.BlockSpec(memory_space=pltpu.HBM)] * 4,
-        out_specs=(pl.BlockSpec(memory_space=pltpu.HBM), pl.BlockSpec(memory_space=VMEM)),
+        out_specs=(pl.BlockSpec(memory_space=VMEM), pl.BlockSpec(memory_space=VMEM)),
         scratch_shapes=[
             VMEM((2 + 2 * bins, wide, rows, LANE), f32),
             VMEM((width, LANE), f32),
@@ -576,7 +569,6 @@
             VMEM((LANE, LANE), f32),
             VMEM((levels, LANE // levels, LANE), f32),
             DMA((2 + 2 * bins,)),
-            DMA((1,)),
             DMA((2, 2)),
             DMA((3, 2, bins)),
             DMA((2, 2)),
@@ -585,13 +577,18 @@
             DMA((2, bins)),
             DMA((2,)),
         ],
-        compiler_params=pltpu.CompilerParams(collective_id=0, has_side_effects=True),
+        compiler_params=pltpu.CompilerParams(collective_id=0, has_side_effects=True, vmem_limit_bytes=32 * 1024 * 1024),
         cost_estimate=pl.CostEstimate(flops=50000000, bytes_accessed=3000000, transcendentals=700000),
     )(
-        tracer.reshape(bins, rows, width),
-        east.reshape(rows, width),
-        north.reshape(rows, width),
-        fall.reshape(bins, rows, width),
+        *(
+            pltpu.with_memory_space_constraint(array, pltpu.HBM)
+            for array in (
+                tracer.reshape(bins, rows, width),
+                east.reshape(rows, width),
+                north.reshape(rows, width),
+                fall.reshape(bins, rows, width),
+            )
+        )
     )
     return out.reshape(tracer.shape), deposit
 

time: 45.6 us -> 42.5 us (0.932)
  the two profiles are of different devices: /device:TPU:112 before, /device:TPU:104 now
where the time goes in v4:
time: 42.5 us; the launch traced here: 42 us
  Pallas kernels  40 us (94%)
  local copies, waits for them, and re-layouts  1.38 us (3%)
  between operations  0.64 us (2%)
    pallas_call x1, Pallas kernels, on_device(): pl.pallas_call(functools.partial(kernel, bands, levels), out_shape=(jax.S...  40 us
    unnamed x2, local copies, waits for them, and re-layouts  1.38 us

profile of v4, /device:TPU:104, one launch (start us, length us, event | category | flops | bytes accessed | tf_op | source)
XLA Modules:
  0.0 42.0 jit_solution(16635122720572716448)
XLA Ops:
  0.6 40.0 %shard_map.59 = (f32[2,48,1152]{2,1,0:T(8,128)S(1)}, f32[2,48,72]{2,1,0:T(8,128)S(1)}) custom-call(f32[2,48,1152]{2,1,0:T(8,128)} %bitcast.8, f32[48,1152]{1,0:T(8,128)} %bitcast.10, f32[48,1152]{1,0:T(8,128)} %bitcast.11, f32[2,48,1152]{2,1,0:T(8,128)} %bitcast.9), custom_call_target="tpu_custom_call" | custom-call | flops 50000000 | bytes 3000000 | tf_op jit(solution)/shard_map/pallas_call | solution.py:537
  40.7 0.8 %copy.9 = f32[2,1,48,1152]{3,2,1,0:T(8,128)} copy(f32[2,1,48,1152]{3,2,1,0:T(8,128)S(1)} %bitcast.7) | data formatting | bytes 884736
  41.4 0.6 %copy.10 = f32[2,48,72]{2,1,0:T(8,128)} copy(f32[2,48,72]{2,1,0:T(8,128)S(1)} %get-tuple-element.11) | data formatting | bytes 55296

commit v5 on v4

--- a/solution.py
+++ b/solution.py
@@ -396,7 +396,7 @@
             for b in range(bins):
                 zonal(e, b, q)
                 send_halo(e, b)
-            send_fall(other_half[3:] + same_half)
+            send_fall(same_half + other_half[3:])
         for b in range(bins):
             meridional_wide(e, b)
             zonal(None, b, q)

time: 42.5 us -> 42.2 us (level)
  no operation moved by 1% of the time
where the time goes in v5:
time: 42.2 us; the launch traced here: 42 us
  Pallas kernels  39.9 us (95%)
  local copies, waits for them, and re-layouts  1.38 us (3%)
  between operations  0.64 us (2%)
    pallas_call x1, Pallas kernels, on_device(): pl.pallas_call(functools.partial(kernel, bands, levels), out_shape=(jax.S...  39.9 us
    unnamed x2, local copies, waits for them, and re-layouts  1.38 us

profile of v5, /device:TPU:104, one launch (start us, length us, event | category | flops | bytes accessed | tf_op | source)
XLA Modules:
  0.0 42.0 jit_solution(7278989354956740429)
XLA Ops:
  0.6 39.9 %shard_map.59 = (f32[2,48,1152]{2,1,0:T(8,128)S(1)}, f32[2,48,72]{2,1,0:T(8,128)S(1)}) custom-call(f32[2,48,1152]{2,1,0:T(8,128)} %bitcast.8, f32[48,1152]{1,0:T(8,128)} %bitcast.10, f32[48,1152]{1,0:T(8,128)} %bitcast.11, f32[2,48,1152]{2,1,0:T(8,128)} %bitcast.9), custom_call_target="tpu_custom_call" | custom-call | flops 50000000 | bytes 3000000 | tf_op jit(solution)/shard_map/pallas_call | solution.py:537
  40.6 0.8 %copy.9 = f32[2,1,48,1152]{3,2,1,0:T(8,128)} copy(f32[2,1,48,1152]{3,2,1,0:T(8,128)S(1)} %bitcast.7) | data formatting | bytes 884736
  41.3 0.6 %copy.10 = f32[2,48,72]{2,1,0:T(8,128)} copy(f32[2,48,72]{2,1,0:T(8,128)S(1)} %get-tuple-element.11) | data formatting | bytes 55296
